TPU v7x, 32 devices: a whole 2x2x4 slice. The times are simulated.
32 devices in a mesh: gx: 2 (over y), gy: 4 (over x, core), gz: 4 (over z).
Axes of the slice: x: 2, y: 2, z: 4, core: 2. Of those that a mesh axis runs over, the one named last changes fastest.
Arguments:
- source: bfloat16 [512, 512, 512], P('gz', 'gx', 'gy'), may hold values from -6 to 6
- forward_x: bfloat16 [512, 512], replicated, may hold values from -0.25 to 0.25
- forward_y: bfloat16 [512, 512], replicated, may hold values from -0.25 to 0.25
- forward_z: bfloat16 [512, 512], replicated, may hold values from -0.25 to 0.25
- inverse_x: bfloat16 [512, 512], replicated, may hold values from -0.25 to 0.25
- inverse_y: bfloat16 [512, 512], replicated, may hold values from -0.25 to 0.25
- inverse_z: bfloat16 [512, 512], replicated, may hold values from -0.25 to 0.25
- values_x: float32 [512], replicated, may hold values from 0.1 to 2
- values_y: float32 [512], replicated, may hold values from 0.1 to 2
- values_z: float32 [512], replicated, may hold values from 0.1 to 2
Outputs:
- solution: bfloat16 [512, 512, 512], P('gz', 'gx', 'gy')
All inputs are finite; a program needn't handle non-finite values.
Results may differ from a plain program's by a relative error of at most 0.015.
Values may be sent and summed in bfloat16 or wider, within the bound.
No kernel may reach another device: no remote copies, remote signals or barrier semaphores. Data moves between devices by JAX's collectives and lax.ppermute only.
A program may use at most 128 MiB of HBM per device.

v0:
```python
import jax
import jax.numpy as jnp
from jax import lax
from jax.sharding import PartitionSpec as P


def along_last(data, basis):
    shape = data.shape
    flat = data.reshape(-1, shape[-1])
    out = lax.dot_general(flat, basis, (((1,), (1,)), ((), ())), preferred_element_type=jnp.float32)
    return out.astype(jnp.bfloat16).reshape(shape[:-1] + (basis.shape[0],))


def along_middle(data, basis):
    out = jnp.einsum("qn,anb->aqb", basis, data, preferred_element_type=jnp.float32)
    return out.astype(jnp.bfloat16)


def along_first(data, basis):
    depth, rows, cols = data.shape
    out = jnp.dot(basis, data.reshape(depth, rows * cols), preferred_element_type=jnp.float32)
    return out.astype(jnp.bfloat16).reshape(basis.shape[0], rows, cols)


def to_plane(block):
    count_y = lax.axis_size("gx")
    count_x = lax.axis_size("gy")
    depth, rows, cols = block.shape
    five = block.reshape(count_y, count_x, depth // (count_x * count_y), rows, cols)
    moved = lax.all_to_all(
        lax.all_to_all(five, "gx", split_axis=0, concat_axis=3, tiled=True),
        "gy",
        split_axis=1,
        concat_axis=4,
        tiled=True,
    )
    return moved.reshape(depth // (count_x * count_y), rows * count_y, cols * count_x)


def from_plane(plane):
    count_y = lax.axis_size("gx")
    count_x = lax.axis_size("gy")
    depth, rows, cols = plane.shape
    five = plane.reshape(1, 1, depth, rows, cols)
    moved = lax.all_to_all(
        lax.all_to_all(five, "gx", split_axis=3, concat_axis=0, tiled=True),
        "gy",
        split_axis=4,
        concat_axis=1,
        tiled=True,
    )
    return moved.reshape(count_y * count_x * depth, rows // count_y, cols // count_x)


def divide(data, values_z, values_y, values_x, y_start, x_start):
    depth, rows, cols = data.shape
    lam_y = lax.dynamic_slice_in_dim(values_y, y_start, rows)
    lam_x = lax.dynamic_slice_in_dim(values_x, x_start, cols)
    denom = values_z[:, None, None] + lam_y[None, :, None] + lam_x[None, None, :]
    return (data.astype(jnp.float32) / denom).astype(jnp.bfloat16)


def on_device(
    source,
    forward_x,
    forward_y,
    forward_z,
    inverse_x,
    inverse_y,
    inverse_z,
    values_x,
    values_y,
    values_z,
):
    depth, rows, cols = source.shape
    index_y = lax.axis_index("gx")
    index_x = lax.axis_index("gy")
    index_z = lax.axis_index("gz")
    plane = to_plane(source)
    step_b = from_plane(along_middle(along_last(plane, forward_x), forward_y))
    lines = lax.all_to_all(step_b, "gz", split_axis=1, concat_axis=0, tiled=True)
    step_c = along_first(lines, forward_z)
    slim = lines.shape[1]
    scaled = divide(
        step_c, values_z, values_y, values_x, index_y * rows + index_z * slim, index_x * cols
    )
    step_d = lax.all_to_all(
        along_first(scaled, inverse_z), "gz", split_axis=0, concat_axis=1, tiled=True
    )
    plane = to_plane(step_d)
    solution = from_plane(along_last(along_middle(plane, inverse_y), inverse_x))
    return solution


def solution(mesh):
    return jax.shard_map(
        on_device,
        mesh=mesh,
        in_specs=(P("gz", "gx", "gy"), P(), P(), P(), P(), P(), P(), P(), P(), P()),
        out_specs=P("gz", "gx", "gy"),
        check_vma=False,
    )
```

profile of v0, /device:TPU:0, one launch (start us, length us, event | category | flops | bytes accessed | tf_op | source)
XLA Modules:
  0.0 1486.8 jit_solution(7768460713005376487)
XLA Ops:
  0.0 0.0 copy-start
  0.0 105.0 %all_to_all.162 = bf16[2,4,16,256,128]{4,3,2,1,0:T(8,128)(2,1)} all-to-all(bf16[2,4,16,256,128]{4,3,2,1,0:T(8,128)(2,1)} %bitcast.107), channel_id=1, replica_groups=mesh['gx'=2,'gy'=4,'gz'=4] {'gx'}, dimensions={0} | all-to-all | bytes 16777216 | tf_op jit(solution)/shard_map/all_to_all | solution.py:31
  105.0 7.9 copy.27
  112.9 100.6 %all_to_all.163 = bf16[1,4,16,512,128]{4,3,2,0,1:T(8,128)(2,1)} all-to-all(bf16[1,4,16,512,128]{4,3,2,0,1:T(8,128)(2,1)} %bitcast.92), channel_id=1, replica_groups=mesh['gx'=2,'gy'=4,'gz'=4] {'gy'}, dimensions={1} | all-to-all | bytes 16777216 | tf_op jit(solution)/shard_map/all_to_all | solution.py:30
  213.5 14.5 copy.29
  228.0 16.4 %copy.48 = bf16[64,8,16,512]{3,1,2,0:T(8,128)(2,1)} copy(bf16[64,8,16,512]{3,2,1,0:T(8,128)(2,1)} %bitcast.94) | data formatting | bytes 16777216
  244.4 0.0 copy-done
  244.4 20.2 %convolution_convert_fusion.3 = bf16[8192,512]{1,0:T(8,128)(2,1)S(1)} fusion(bf16[8192,512]{0,1:T(8,128)(2,1)} %bitcast.108, bf16[512,512]{1,0:T(8,128)(2,1)S(1)} %copy-done), kind=kOutput, calls=%fused_computation.6 | convolution fusion | flops 4299161600 | bytes 17301504 | tf_op jit(solution)/shard_map/dot_general | solution.py:10
  264.6 0.0 copy-done.4
  264.6 6.9 convert_bitcast_fusion
  271.6 14.9 %copy.31 = bf16[1,1,16,512,512]{4,2,1,0,3:T(8,128)(2,1)} copy(bf16[1,1,16,512,512]{3,4,2,1,0:T(8,128)(2,1)} %convert_bitcast_fusion) | data formatting | bytes 16777216 | tf_op jit(solution)/shard_map/reshape | solution.py:44
  286.5 103.3 %all_to_all.164 = bf16[1,1,16,512,512]{4,2,1,0,3:T(8,128)(2,1)} all-to-all(bf16[1,1,16,512,512]{4,2,1,0,3:T(8,128)(2,1)} %copy.31), channel_id=1, replica_groups=mesh['gx'=2,'gy'=4,'gz'=4] {'gx'}, dimensions={3} | all-to-all | bytes 16777216 | tf_op jit(solution)/shard_map/all_to_all | solution.py:46
  389.7 15.8 %copy.32 = bf16[1,1,16,2,256,512]{4,2,3,5,1,0:T(8,128)(2,1)} copy(bf16[1,1,16,2,256,512]{5,2,4,3,1,0:T(8,128)(2,1)} %bitcast.95) | data formatting | bytes 16777216 | tf_op jit(solution)/shard_map/all_to_all | solution.py:46
  405.6 100.6 %all_to_all.165 = bf16[2,1,16,256,512]{3,2,0,1,4:T(8,128)(2,1)} all-to-all(bf16[2,1,16,256,512]{3,2,0,1,4:T(8,128)(2,1)} %bitcast.96), channel_id=1, replica_groups=mesh['gx'=2,'gy'=4,'gz'=4] {'gy'}, dimensions={4} | all-to-all | bytes 16777216 | tf_op jit(solution)/shard_map/all_to_all | solution.py:45
  506.2 11.5 copy.33
  517.7 11.4 copy.34
  529.1 12.2 copy.35
  541.3 6.2 all-to-all-start.4
  547.5 0.8 dynamic_slice.6
  548.3 0.8 dynamic_slice.7
  549.0 0.0 copy-done.3
  549.0 0.1 broadcast_add_fusion
  549.1 181.5 %all-to-all-done.4 = bf16[128,256,128]{2,0,1:T(8,128)(2,1)} async-done(((bf16[128,256,128]{2,0,1:T(8,128)(2,1)}), bf16[128,256,128]{2,0,1:T(8,128)(2,1)}, u32[]{:S(2)}, u32[]{:S(2)}) %all-to-all-start.4) | async-done | bytes 8388640 | tf_op jit(solution)/shard_map/all_to_all | solution.py:81
  730.6 12.3 copy.36
  742.9 0.0 copy-done.2
  742.9 10.9 fusion.1
  753.8 0.0 copy-done.5
  753.8 6.8 convolution_convert_fusion.1
  760.6 12.1 copy.37
  772.6 190.1 %all_to_all.166 = bf16[512,64,128]{2,1,0:T(8,128)(2,1)} all-to-all(bf16[512,64,128]{2,1,0:T(8,128)(2,1)} %copy.37), channel_id=1, replica_groups=mesh['gx'=2,'gy'=4,'gz'=4] {'gz'}, dimensions={0} | all-to-all | bytes 16777216 | tf_op jit(solution)/shard_map/all_to_all | solution.py:87
  962.7 9.8 copy.38
  972.5 102.3 %all_to_all.167 = bf16[2,4,16,256,128]{4,3,2,1,0:T(8,128)(2,1)} all-to-all(bf16[2,4,16,256,128]{4,3,2,1,0:T(8,128)(2,1)} %bitcast.100), channel_id=1, replica_groups=mesh['gx'=2,'gy'=4,'gz'=4] {'gx'}, dimensions={0} | all-to-all | bytes 16777216 | tf_op jit(solution)/shard_map/all_to_all | solution.py:31
  1074.8 7.9 copy.39
  1082.7 97.4 %all_to_all.168 = bf16[1,4,16,512,128]{4,3,2,0,1:T(8,128)(2,1)S(1)} all-to-all(bf16[1,4,16,512,128]{4,3,2,0,1:T(8,128)(2,1)} %bitcast.102), channel_id=1, replica_groups=mesh['gx'=2,'gy'=4,'gz'=4] {'gy'}, dimensions={1} | all-to-all | bytes 16777216 | tf_op jit(solution)/shard_map/all_to_all | solution.py:30
  1180.1 7.4 copy.41
  1187.5 13.2 reshape.80
  1200.7 0.0 copy-done.6
  1200.7 8.2 convolution_convert_fusion.4
  1208.9 0.0 copy-done.7
  1208.9 6.8 convolution_convert_fusion
  1215.7 11.3 copy.42
  1227.0 103.5 %all_to_all.169 = bf16[1,1,16,512,512]{4,2,1,0,3:T(8,128)(2,1)} all-to-all(bf16[1,1,16,512,512]{4,2,1,0,3:T(8,128)(2,1)} %copy.42), channel_id=1, replica_groups=mesh['gx'=2,'gy'=4,'gz'=4] {'gx'}, dimensions={3} | all-to-all | bytes 16777216 | tf_op jit(solution)/shard_map/all_to_all | solution.py:46
  1330.5 11.5 copy.43
  1342.0 21.2 %copy.44 = bf16[2,1,16,256,512]{3,0,2,1,4:T(2,128)(2,1)} copy(bf16[2,1,16,256,512]{4,3,0,2,1:T(8,128)(2,1)} %bitcast.104) | data formatting | bytes 16777216 | tf_op jit(solution)/shard_map/all_to_all | solution.py:46
  1363.2 100.6 %all_to_all.170 = bf16[2,1,16,256,512]{3,0,2,1,4:T(2,128)(2,1)} all-to-all(bf16[2,1,16,256,512]{3,0,2,1,4:T(2,128)(2,1)} %copy.44), channel_id=1, replica_groups=mesh['gx'=2,'gy'=4,'gz'=4] {'gy'}, dimensions={4} | all-to-all | bytes 16777216 | tf_op jit(solution)/shard_map/all_to_all | solution.py:45
  1463.8 11.4 copy.45
  1475.1 11.4 copy.46
  1486.6 0.0 copy-done.1
  (8 shorter events, 0.0 us)
Async XLA Ops:
  0.0 244.4 %copy-start = (bf16[512,512]{1,0:T(8,128)(2,1)S(1)}, bf16[512,512]{1,0:T(8,128)(2,1)}, u32[]{:S(2)}) copy-start(bf16[512,512]{1,0:T(8,128)(2,1)} %param.11) | copy-start | bytes 1572868
  244.4 20.2 %copy-start.4 = (bf16[512,512]{1,0:T(8,128)(2,1)S(1)}, bf16[512,512]{1,0:T(8,128)(2,1)}, u32[]{:S(2)}) copy-start(bf16[512,512]{1,0:T(8,128)(2,1)} %param.12) | copy-start | bytes 1572868
  541.3 7.7 copy-start.3
  541.3 189.3 %all-to-all-start.4 = ((bf16[128,256,128]{2,0,1:T(8,128)(2,1)}), bf16[128,256,128]{2,0,1:T(8,128)(2,1)}, u32[]{:S(2)}, u32[]{:S(2)}) async-start(bf16[128,256,128]{2,0,1:T(8,128)(2,1)} %copy.35), calls=%async_computation.4 | async-start | bytes 16777216 | tf_op jit(solution)/shard_map/all_to_all | solution.py:81
  730.6 12.3 copy-start.2
  742.9 10.9 copy-start.5
  1187.5 13.2 copy-start.6
  1200.7 8.2 copy-start.7
  1475.1 11.4 copy-start.1
where the time goes:
time: 1500 us; the launch traced here: 1490 us
  blocking collectives  1000 us (67%)
  local copies, waits for them, and re-layouts  236 us (16%)
  waiting for transfers between devices  182 us (12%)
  matrix products  59.8 us (4%)
    all_to_all x2, blocking collectives, to_plane(): lax.all_to_all(five, 'gx', split_axis=0, concat_axis=3, tiled=True)  207 us
    all_to_all x2, blocking collectives, from_plane(): lax.all_to_all(five, 'gx', split_axis=3, concat_axis=0, tiled=True)  207 us
    all_to_all x2, blocking collectives, from_plane(): lax.all_to_all(lax.all_to_all(five, 'gx', split_axis=3, concat_axis=0, ti...  201 us
    all_to_all x2, blocking collectives, to_plane(): lax.all_to_all(lax.all_to_all(five, 'gx', split_axis=0, concat_axis=3, ti...  198 us
    all_to_all x1, blocking collectives, on_device(): lax.all_to_all(along_first(scaled, inverse_z), 'gz', split_axis=0, concat...  190 us
    all_to_all x1, waiting for transfers between devices, on_device(): lax.all_to_all(step_b, 'gz', split_axis=1, concat_axis=0, tiled=True)  182 us
    all_to_all x3, local copies, waits for them, and re-layouts, from_plane(): lax.all_to_all(five, 'gx', split_axis=3, concat_axis=0, tiled=True)  48.6 us
    all_to_all x4, local copies, waits for them, and re-layouts, from_plane(): lax.all_to_all(lax.all_to_all(five, 'gx', split_axis=3, concat_axis=0, ti...  45.8 us
  transfers between devices with their start and end apart: 1, of which 1 were waited for; matrix products, arithmetic and copies ran while one was open for 0% of the time, Pallas kernels for 0%

commit v1 on v0

v1 whole, which is shorter than its diff:
```python
import functools

import jax
import jax.numpy as jnp
from jax import lax
from jax.experimental import pallas as pl
from jax.experimental.pallas import tpu as pltpu
from jax.sharding import PartitionSpec as P


FORWARD_SIZES = (1,)*8
BACKWARD_SIZES = (1,)*8
AHEAD = {'S':2,'W':2}
SENDS = {"S": "gx", "G": "gy", "Z": "gz", "W": "gz", "H": "gy", "T": "gx"}
ROWS = 8
F32 = jnp.float32
BF16 = jnp.bfloat16


def dot(a, b):
    return jnp.dot(a, b, preferred_element_type=F32)


def params(**kw):
    return pltpu.CompilerParams(vmem_limit_bytes=48 * 1024 * 1024, **kw)


def cost(flops, nbytes):
    return pl.CostEstimate(flops=flops, bytes_accessed=nbytes, transcendentals=0)


ANY = pl.BlockSpec(memory_space=pl.ANY)


def chunks(depth, sizes):
    rows = [n * depth // sum(sizes) for n in sizes]
    by_z = [0, len(rows) - 1] + list(range(1, len(rows) - 1))
    starts = [0] * len(rows)
    for a, b in zip(by_z, by_z[1:]):
        starts[b] = starts[a] + rows[a]
    return rows, starts, by_z


def forward_order():
    n = len(FORWARD_SIZES)
    ahead = AHEAD["S"]
    steps = [f"{kind}{c}" for c in range(ahead) for kind in "CS"]
    for c in range(n):
        steps += [f"F{c}", f"G{c}"]
        steps += [f"{kind}{c + ahead}" for kind in "CS" if c + ahead < n]
        steps += [f"A{c}", f"Z{c}"]
    return steps


def backward_order():
    n = len(BACKWARD_SIZES)
    steps = [f"W{c}" for c in range(AHEAD["W"])]
    for c in range(n):
        steps += [f"B{c}", f"H{c}"] + [f"W{c + AHEAD['W']}"] * (c + AHEAD["W"] < n)
        steps += [f"P{c}", f"T{c}"] + [f"R{c - 2}"] * (c > 1)
    return steps + [f"R{n - 2}", f"R{n - 1}"]


def partners(count):
    return list(range(2, count)) + [1]


def places(index, count):
    return [index ^ k for k in range(count)]


def cut(ref, height, row, width, col):
    return ref[
        pl.ds(pl.multiple_of(row * height, height), height),
        pl.ds(pl.multiple_of(col * width, width), width),
    ]


def forward_y_kernel(*refs, count, outs):
    place, pieces, basis, out = refs[0], refs[1 : 1 + count], refs[1 + count], refs[-outs:]
    steps, rows, cols = pieces[0].shape
    width = basis.shape[0] // count // outs
    own = jnp.concatenate(
        [
            jnp.concatenate([cut(basis, width, r, rows, c) for c in places(place[0], count)], axis=1)
            for r in places(place[0] * outs + place[1], outs)
        ],
        axis=0,
    )

    def pair(i, carry):
        z = 2 * i
        rhs = jnp.concatenate(
            [jnp.concatenate([ref[z], ref[z + 1]], axis=1) for ref in pieces], axis=0
        )
        acc = dot(own, rhs).astype(BF16)
        for k in range(outs):
            block = acc[k * width : (k + 1) * width]
            out[k][z] = block[:, :cols]
            out[k][z + 1] = block[:, cols:]
        return carry

    lax.fori_loop(0, steps // 2, pair, 0, unroll=4)


def forward_y(place, own, start, others, basis, outs, after=()):
    zc, rows, cols = others[0].shape
    count = 1 + len(others)
    q = basis.shape[0] // count
    first = start // ROWS
    spec = pl.BlockSpec((ROWS, rows, cols), lambda i, s: (i, 0, 0))
    return pl.pallas_call(
        functools.partial(forward_y_kernel, count=count, outs=outs),
        grid_spec=pltpu.PrefetchScalarGridSpec(
            num_scalar_prefetch=1,
            grid=(zc // ROWS,),
            in_specs=[pl.BlockSpec((ROWS, rows, cols), lambda i, s: (i + first, 0, 0))]
            + [spec] * len(others)
            + [pl.BlockSpec(basis.shape, lambda i, s: (0, 0))]
            + [ANY] * len(after),
            out_specs=[pl.BlockSpec((ROWS, q // outs, cols), lambda i, s: (i, 0, 0))] * outs,
        ),
        out_shape=[jax.ShapeDtypeStruct((zc, q // outs, cols), BF16)] * outs,
        compiler_params=params(),
        cost_estimate=cost(2 * zc * q * basis.shape[1] * cols, 2 * zc * cols * (basis.shape[1] + q)),
        name="forward_y",
    )(place, own, *others, basis, *after)


def along_x_kernel(*refs, count, outs, axes):
    place, pieces, basis = refs[0], refs[1 : 1 + count], refs[1 + count]
    out, scratch = refs[-1 - outs : -1], refs[-1]
    a, b, cols = pieces[0].shape
    pitch = scratch.shape[1] // a
    width = basis.shape[0] // outs
    lhs = jnp.concatenate([ref[...].reshape(a * b, cols) for ref in pieces], axis=1)
    for k, row in enumerate(places(place[axes[1]], outs)):
        rhs = jnp.concatenate(
            [cut(basis, width, row, cols, c) for c in places(place[axes[0]], count)], axis=1
        )
        acc = lax.dot_general(lhs, rhs, (((1,), (1,)), ((), ())), preferred_element_type=F32)
        for i in range(a):
            scratch[k % 2, i * pitch : i * pitch + b, :] = acc[i * b : (i + 1) * b]
        for j in range(b):
            out[k][j] = scratch[k % 2, pl.ds(j, a, stride=pitch), :].astype(BF16)


def along_x(place, pieces, basis, outs, rows_first, after=()):
    cols = pieces[0].shape[2]
    width = basis.shape[0] // outs
    zc, q = pieces[0].shape[:2] if rows_first else pieces[0].shape[1::-1]
    z_major = ((ROWS, q), lambda i, s: (i, 0, 0))
    q_major = ((q, ROWS), lambda i, s: (0, i, 0))
    src, dst = (z_major, q_major) if rows_first else (q_major, z_major)
    shape = (q, zc, width) if rows_first else (zc, q, width)
    pitch = src[0][1] + 8
    return pl.pallas_call(
        functools.partial(
            along_x_kernel, count=len(pieces), outs=outs, axes=(1, 2) if rows_first else (2, 1)
        ),
        grid_spec=pltpu.PrefetchScalarGridSpec(
            num_scalar_prefetch=1,
            grid=(zc // ROWS,),
            in_specs=[pl.BlockSpec(src[0] + (cols,), src[1])] * len(pieces)
            + [pl.BlockSpec(basis.shape, lambda i, s: (0, 0))]
            + [ANY] * len(after),
            out_specs=[pl.BlockSpec(dst[0] + (width,), dst[1])] * outs,
            scratch_shapes=[pltpu.VMEM((2, src[0][0] * pitch, width), F32)],
        ),
        out_shape=[jax.ShapeDtypeStruct(shape, BF16)] * outs,
        compiler_params=params(),
        cost_estimate=cost(2 * zc * q * basis.shape[0] * basis.shape[1], 2 * zc * q * sum(basis.shape)),
        name="along_x",
    )(place, *pieces, basis, *after)


def lines_kernel(*refs, count, outs, step):
    place, lam_y, pieces = refs[0], refs[1], refs[2 : 2 + count]
    forward, inverse, base = refs[2 + count : 5 + count]
    out, there, back_again = refs[-2 - outs : -2], refs[-2], refs[-1]
    first = pl.program_id(0) * step
    depth, cols = base.shape

    @pl.when(pl.program_id(0) == 0)
    def _():
        n = there.shape[0]
        size = depth // n
        for k, block in enumerate(places(place[2], n)):
            there[k] = forward[:, pl.ds(pl.multiple_of(block * size, size), size)]
            back_again[k * size : (k + 1) * size] = inverse[pl.ds(pl.multiple_of(block * size, size), size), :]

    lhs = jnp.concatenate([there[k] for k in range(there.shape[0])], axis=1)
    for q in range(0, step, 2):
        rhs = jnp.concatenate(
            [jnp.concatenate([ref[q], ref[q + 1]], axis=1) for ref in pieces], axis=0
        )
        acc = dot(lhs, rhs).astype(BF16).astype(F32)
        left = acc[:, :cols] / (base[...] + lam_y[first + q])
        right = acc[:, cols:] / (base[...] + lam_y[first + q + 1])
        back = dot(back_again[...], jnp.concatenate([left, right], axis=1).astype(BF16)).astype(BF16)
        row = 0
        for ref in out:
            stop = row + ref.shape[1]
            ref[q] = back[row:stop, :cols]
            ref[q + 1] = back[row:stop, cols:]
            row = stop


def lines(place, pieces, forward, inverse, base, lam_y, parts, sizes):
    q, _, cols = pieces[0].shape
    depth = forward.shape[0]
    step = 8
    spec = lambda n: pl.BlockSpec((step, n, cols), lambda i, s, t: (i, 0, 0))
    whole = lambda x: pl.BlockSpec(x.shape, lambda i, s, t: (0, 0))
    outs = [n for _ in range(parts) for n in sizes]
    return pl.pallas_call(
        functools.partial(lines_kernel, count=len(pieces), outs=len(outs), step=step),
        grid_spec=pltpu.PrefetchScalarGridSpec(
            num_scalar_prefetch=2,
            grid=(q // step,),
            in_specs=[spec(p.shape[1]) for p in pieces] + [whole(forward), whole(inverse), whole(base)],
            out_specs=[spec(n) for n in outs],
            scratch_shapes=[
                pltpu.VMEM((parts, depth, depth // parts), BF16),
                pltpu.VMEM((depth, depth), BF16),
            ],
        ),
        out_shape=[jax.ShapeDtypeStruct((q, n, cols), BF16) for n in outs],
        compiler_params=params(),
        cost_estimate=cost(4 * q * cols * depth * depth, 4 * q * cols * depth),
        name="lines",
    )(place, lam_y, *pieces, forward, inverse, base)


def inverse_y_kernel(*refs, count, adds, to):
    place, pieces, basis = refs[0], refs[1 : 1 + count], refs[1 + count]
    partials, out, there = refs[2 + count : 2 + count + adds], refs[-2], refs[-1]
    _, q, cols = pieces[0].shape
    rows = out.shape[1]
    own = cut(basis, rows, place[0] ^ to, count * q, place[0])
    for ref, k in zip(pieces, places(place[1], count)):
        there[k] = ref[...]

    def pair(i, carry):
        z = 2 * i
        rhs = jnp.concatenate(
            [jnp.concatenate([there[k, z], there[k, z + 1]], axis=1) for k in range(count)], axis=0
        )
        acc = dot(own, rhs)
        left, right = acc[:, :cols], acc[:, cols:]
        for ref in partials:
            left = left + ref[z].astype(F32)
            right = right + ref[z + 1].astype(F32)
        out[z] = left.astype(BF16)
        out[z + 1] = right.astype(BF16)
        return carry

    lax.fori_loop(0, out.shape[0] // 2, pair, 0, unroll=4)


def inverse_y(place, pieces, basis, to, rows, after=(), partials=(), into=None, start=0, depth=None):
    zc, q, cols = pieces[0].shape
    first = start // ROWS
    part = pl.BlockSpec((ROWS, rows, cols), lambda i, s: (i, 0, 0))
    extra = [] if into is None else [into]
    count = len(pieces)
    return pl.pallas_call(
        functools.partial(inverse_y_kernel, count=count, adds=len(partials), to=to),
        grid_spec=pltpu.PrefetchScalarGridSpec(
            num_scalar_prefetch=1,
            grid=(zc // ROWS,),
            in_specs=[pl.BlockSpec((ROWS, q, cols), lambda i, s: (i, 0, 0))] * count
            + [pl.BlockSpec(basis.shape, lambda i, s: (0, 0))]
            + [part] * len(partials)
            + [ANY] * (len(extra) + len(after)),
            out_specs=pl.BlockSpec((ROWS, rows, cols), lambda i, s: (i + first, 0, 0)),
            scratch_shapes=[pltpu.VMEM((count, ROWS, q, cols), BF16)],
        ),
        out_shape=jax.ShapeDtypeStruct((depth or zc, rows, cols), BF16),
        input_output_aliases={count + 2 + len(partials): 0} if extra else {},
        compiler_params=params(),
        cost_estimate=cost(2 * zc * rows * count * q * cols, 2 * zc * cols * (count * q + rows)),
        name="inverse_y",
    )(place, *pieces, basis, *partials, *extra, *after)


def swap(value, axis, k):
    count = lax.axis_size(axis)
    return lax.ppermute(value, axis, [(i, i ^ k) for i in range(count)])


def exchange(step, pieces):
    axis = SENDS[step[0]]
    out = list(pieces)
    for k in partners(len(pieces)):
        out[k] = swap(pieces[k], axis, k)
    return out


def copy_kernel(source, out):
    out[...] = source[...]


def copy_rows(source, start, count):
    first = start // ROWS
    block = (ROWS,) + source.shape[1:]
    return pl.pallas_call(
        copy_kernel,
        grid=(count // block[0],),
        in_specs=[pl.BlockSpec(block, lambda i: (i + first, 0, 0))],
        out_specs=pl.BlockSpec(block, lambda i: (i, 0, 0)),
        out_shape=jax.ShapeDtypeStruct((count,) + source.shape[1:], BF16),
        compiler_params=params(),
        name="copy_rows",
    )(source)


def on_device(
    source, forward_x, forward_y_basis, forward_z, inverse_x, inverse_y_basis, inverse_z,
    values_x, values_y, values_z,
):
    ny, ng, nz = lax.axis_size("gx"), lax.axis_size("gy"), lax.axis_size("gz")
    iy, ig, iz = lax.axis_index("gx"), lax.axis_index("gy"), lax.axis_index("gz")
    place = jnp.stack([iy, ig, iz]).astype(jnp.int32)
    depth, rows, _ = source.shape
    slim = values_y.shape[0] // ny // ng
    width = values_x.shape[0] // nz
    lam_y = lax.dynamic_slice_in_dim(values_y, (iy * ng + ig) * slim, slim)
    lam_x = lax.dynamic_slice_in_dim(values_x, iz * width, width)
    base = values_z[:, None] + lam_x[None, :]

    sizes, starts, by_z = chunks(depth, FORWARD_SIZES)
    have = {}
    for step in forward_order():
        kind, c = step[0], int(step[1:])
        if kind in "CFA":
            if kind == "C":
                have[step] = copy_rows(source, starts[c], sizes[c])
            elif kind == "F":
                have[step] = forward_y(
                    place, source, starts[c], have[f"S{c}"], forward_y_basis, ng
                )
            else:
                have[step] = along_x(place, have[f"G{c}"], forward_x, nz, True)
        elif kind == "S":
            have[step] = exchange(step, [have[f"C{c}"]] * ny)[1:]
        else:
            have[step] = exchange(step, have[f"{'F' if kind == 'G' else 'A'}{c}"])

    flat = [have[f"Z{c}"][k] for k in range(nz) for c in by_z]
    sizes, starts, by_z = chunks(depth, BACKWARD_SIZES)
    count = len(sizes)
    flat = lines(place, flat, forward_z, inverse_z, base, lam_y, nz, [sizes[c] for c in by_z])

    result = None
    for step in backward_order():
        kind, c = step[0], int(step[1:])
        if kind == "W":
            have[step] = exchange(step, [flat[k * count + by_z.index(c)] for k in range(nz)])
        elif kind == "H":
            have[step] = exchange(step, have[f"B{c}"])
        elif kind == "T":
            have[step] = exchange(step, [None] + have[f"P{c}"])[1:]
        elif kind == "P":
            have[step] = [None] * (ny - 1)
            for k in partners(ny):
                have[step][k - 1] = inverse_y(place, have[f"H{c}"], inverse_y_basis, k, rows)
        else:
            if kind == "B":
                have[step] = along_x(place, have[f"W{c}"], inverse_x, ng, False)
            else:
                result = inverse_y(
                    place, have[f"H{c}"], inverse_y_basis, 0, rows, (),
                    have[f"T{c}"], result, starts[c], depth,
                )
    return result


def plain(data, basis, spec):
    return jnp.einsum(spec, basis, data, preferred_element_type=F32).astype(BF16)


def on_device_plain(
    source, forward_x, forward_y_basis, forward_z, inverse_x, inverse_y_basis, inverse_z,
    values_x, values_y, values_z,
):
    iy, ig, iz = lax.axis_index("gx"), lax.axis_index("gy"), lax.axis_index("gz")
    move = functools.partial(lax.all_to_all, tiled=True)
    step = move(source, "gx", split_axis=0, concat_axis=1)
    step = move(plain(step, forward_y_basis, "qy,zyx->zqx"), "gx", split_axis=1, concat_axis=0)
    step = move(step, "gy", split_axis=1, concat_axis=2)
    step = plain(step, forward_x, "px,zqx->zqp")
    step = plain(move(step, "gz", split_axis=2, concat_axis=0), forward_z, "rz,zqp->rqp")
    _, rows, cols = step.shape
    first = (iy * lax.axis_size("gy") + ig) * rows
    lam_y = lax.dynamic_slice_in_dim(values_y, first, rows)
    lam_x = lax.dynamic_slice_in_dim(values_x, iz * cols, cols)
    denom = values_z[:, None, None] + lam_y[None, :, None] + lam_x[None, None, :]
    step = (step.astype(F32) / denom).astype(BF16)
    step = move(plain(step, inverse_z, "zr,rqp->zqp"), "gz", split_axis=0, concat_axis=2)
    step = plain(step, inverse_x, "xp,zqp->zqx")
    step = move(step, "gy", split_axis=2, concat_axis=1)
    step = move(step, "gx", split_axis=0, concat_axis=1)
    return move(plain(step, inverse_y_basis, "yq,zqx->zyx"), "gx", split_axis=1, concat_axis=0)


def solution(mesh):
    def run(source, *rest):
        ny, ng, nz = (mesh.shape[a] for a in ("gx", "gy", "gz"))
        depth, size_y, size_x = source.shape
        fits = (
            size_x // nz % 128 == 0
            and size_x // ng % 128 == 0
            and depth // nz % (ROWS * sum(FORWARD_SIZES)) == 0
            and depth // nz % (ROWS * sum(BACKWARD_SIZES)) == 0
            and size_y // ny // ng % 16 == 0
            and all(n & (n - 1) == 0 for n in (ny, ng, nz))
        )
        body = on_device_plain
        if fits:

            def body(*args):
                return on_device(*args)

        step = jax.shard_map(
            body,
            mesh=mesh,
            in_specs=(P("gz", "gx", "gy"),) + (P(),) * 9,
            out_specs=P("gz", "gx", "gy"),
            check_vma=False,
        )
        return step(source, *rest)

    return run
```

time: 1500 us -> 889 us (0.59)
  blocking collectives: 1000 us -> 0 us
  waiting for transfers between devices: 182 us -> 537 us
  local copies, waits for them, and re-layouts: 236 us -> 14.9 us
  starting transfers between devices: 6.18 us -> 212 us
  Pallas kernels: 0 us -> 124 us
  matrix products: 59.8 us -> 0 us
    all_to_all x9 -> x0, blocking collectives: 1000 us -> none  [the longest x2 207 us: to_plane(): lax.all_to_all(five, 'gx', split_axis=0, concat_axis=3, tiled=True)]
    ppermute x0 -> x112, waiting for transfers between devices: none -> 537 us  [swap(): return lax.ppermute(value, axis, [(i, i ^ k) for i in range(count)])]
    ppermute x0 -> x112, starting transfers between devices: none -> 212 us  [swap(): return lax.ppermute(value, axis, [(i, i ^ k) for i in range(count)])]
    all_to_all x1 -> x0, waiting for transfers between devices: 182 us -> none  [on_device(): lax.all_to_all(step_b, 'gz', split_axis=1, concat_axis=0, tiled=True)]
    all_to_all x13 -> x0, local copies, waits for them, and re-layouts: 154 us -> none  [the longest x3 48.6 us: from_plane(): lax.all_to_all(five, 'gx', split_axis=3, concat_axis=0, tiled=True)]
    pallas_call x0 -> x49, Pallas kernels: none -> 124 us  [the longest x16 39.5 us: along_x(): pl.pallas_call(functools.partial(along_x_kernel, count=len(pieces), outs=...]
    dot_general x6 -> x0, matrix products: 59.8 us -> none  [the longest x2 27 us: along_last(): lax.dot_general(flat, basis, (((1,), (1,)), ((), ())), preferred_element_...]
    reshape x4 -> x0, local copies, waits for them, and re-layouts: 52.3 us -> none  [the longest x1 14.9 us: from_plane(): five = plane.reshape(1, 1, depth, rows, cols)]
  transfers between devices with their start and end apart: 1 -> 112, of which waited for: 1 -> 55; matrix products, arithmetic and copies ran while one was open for 0% -> 0% of each run, Pallas kernels for 0% -> 12%
where the time goes in v1:
time: 889 us
  waiting for transfers between devices  537 us (60%)
  starting transfers between devices  212 us (24%)
  Pallas kernels  124 us (14%)
  local copies, waits for them, and re-layouts  14.9 us (2%)
    ppermute x112, waiting for transfers between devices, swap(): return lax.ppermute(value, axis, [(i, i ^ k) for i in range(count)])  537 us
    ppermute x112, starting transfers between devices, swap(): return lax.ppermute(value, axis, [(i, i ^ k) for i in range(count)])  212 us
    pallas_call x16, Pallas kernels, along_x(): pl.pallas_call(functools.partial(along_x_kernel, count=len(pieces), outs=...  39.5 us
    pallas_call x16, Pallas kernels, inverse_y(): pl.pallas_call(functools.partial(inverse_y_kernel, count=count, adds=len(...  32.6 us
    pallas_call x8, Pallas kernels, forward_y(): pl.pallas_call(functools.partial(forward_y_kernel, count=count, outs=outs...  20.6 us
  transfers between devices with their start and end apart: 112, of which 55 were waited for; matrix products, arithmetic and copies ran while one was open for 0% of the time, Pallas kernels for 12%

profile of v1, /device:TPU:0, one launch (start us, length us, event | category | flops | bytes accessed | tf_op | source)
XLA Modules:
  0.0 888.6 jit_solution(15687384552648190790)
XLA Ops:
  17.2 11.1 %collective-permute-done.8.refs_2_ = bf16[16,256,128]{2,1,0:T(8,128)(2,1)S(1)} collective-permute-done((bf16[16,256,128]{2,1,0:T(8,128)(2,1)S(1)}, bf16[16,256,128]{2,1,0:T(8,128)(2,1)S(1)}, u32[]{:S(2)}, u32[]{:S(2)}) %collective-permute-start.8) | collective-permute-done | bytes 1048608 | tf_op jit(solution)/shard_map/ppermute | solution.py:289
  32.5 18.3 %collective-permute-done.12.refs_2_ = bf16[16,256,128]{2,1,0:T(8,128)(2,1)S(1)} collective-permute-done((bf16[16,256,128]{2,1,0:T(8,128)(2,1)S(1)}, bf16[16,256,128]{2,1,0:T(8,128)(2,1)S(1)}, u32[]{:S(2)}, u32[]{:S(2)}) %collective-permute-start.12) | collective-permute-done | bytes 1048608 | tf_op jit(solution)/shard_map/ppermute | solution.py:289
  54.9 18.4 %collective-permute-done.16.refs_2_ = bf16[16,256,128]{2,1,0:T(8,128)(2,1)S(1)} collective-permute-done((bf16[16,256,128]{2,1,0:T(8,128)(2,1)S(1)}, bf16[16,256,128]{2,1,0:T(8,128)(2,1)S(1)}, u32[]{:S(2)}, u32[]{:S(2)}) %collective-permute-start.16) | collective-permute-done | bytes 1048608 | tf_op jit(solution)/shard_map/ppermute | solution.py:289
  80.2 15.7 %collective-permute-done.20.refs_2_ = bf16[16,256,128]{2,1,0:T(8,128)(2,1)} collective-permute-done((bf16[16,256,128]{2,1,0:T(8,128)(2,1)}, bf16[16,256,128]{2,1,0:T(8,128)(2,1)}, u32[]{:S(2)}, u32[]{:S(2)}) %collective-permute-start.20) | collective-permute-done | bytes 1048608 | tf_op jit(solution)/shard_map/ppermute | solution.py:289
  97.8 20.5 %collective-permute-done.24.refs_2_ = bf16[16,256,128]{2,1,0:T(8,128)(2,1)} collective-permute-done((bf16[16,256,128]{2,1,0:T(8,128)(2,1)}, bf16[16,256,128]{2,1,0:T(8,128)(2,1)}, u32[]{:S(2)}, u32[]{:S(2)}) %collective-permute-start.24) | collective-permute-done | bytes 1048608 | tf_op jit(solution)/shard_map/ppermute | solution.py:289
  118.3 22.5 %collective-permute-done.28.refs_2_ = bf16[16,256,128]{2,1,0:T(8,128)(2,1)} collective-permute-done((bf16[16,256,128]{2,1,0:T(8,128)(2,1)}, bf16[16,256,128]{2,1,0:T(8,128)(2,1)}, u32[]{:S(2)}, u32[]{:S(2)}) %collective-permute-start.28) | collective-permute-done | bytes 1048608 | tf_op jit(solution)/shard_map/ppermute | solution.py:289
  145.8 17.3 %collective-permute-done.4.refs_2_ = bf16[16,256,128]{2,1,0:T(8,128)(2,1)S(1)} collective-permute-done((bf16[16,256,128]{2,1,0:T(8,128)(2,1)}, bf16[16,256,128]{2,1,0:T(8,128)(2,1)S(1)}, u32[]{:S(2)}, u32[]{:S(2)}) %collective-permute-start.4) | collective-permute-done | bytes 1048608 | tf_op jit(solution)/shard_map/ppermute | solution.py:289
  163.2 21.6 %collective-permute-done.refs_2_ = bf16[16,256,128]{2,1,0:T(8,128)(2,1)S(1)} collective-permute-done((bf16[16,256,128]{2,1,0:T(8,128)(2,1)}, bf16[16,256,128]{2,1,0:T(8,128)(2,1)S(1)}, u32[]{:S(2)}, u32[]{:S(2)}) %collective-permute-start) | collective-permute-done | bytes 1048608 | tf_op jit(solution)/shard_map/ppermute | solution.py:289
  216.4 4.8 collective-permute-done.23.refs_4_
  238.9 4.8 collective-permute-done.31.refs_4_
  274.8 8.4 collective-permute-done.36.refs_14_
  285.1 9.3 %collective-permute-done.37.refs_15_ = bf16[64,16,128]{2,1,0:T(8,128)(2,1)S(1)} collective-permute-done((bf16[64,16,128]{2,1,0:T(8,128)(2,1)S(1)}, bf16[64,16,128]{2,1,0:T(8,128)(2,1)S(1)}, u32[]{:S(2)}, u32[]{:S(2)}) %collective-permute-start.37) | collective-permute-done | bytes 262176 | tf_op jit(solution)/shard_map/ppermute | solution.py:289
  311.5 29.2 %collective-permute-done.44.refs_22_ = bf16[64,16,128]{2,1,0:T(8,128)(2,1)S(1)} collective-permute-done((bf16[64,16,128]{2,1,0:T(8,128)(2,1)S(1)}, bf16[64,16,128]{2,1,0:T(8,128)(2,1)S(1)}, u32[]{:S(2)}, u32[]{:S(2)}) %collective-permute-start.44) | collective-permute-done | bytes 262176 | tf_op jit(solution)/shard_map/ppermute | solution.py:289
  344.8 7.2 collective-permute-done.45.refs_23_
  353.3 9.9 %collective-permute-done.46.refs_24_ = bf16[64,16,128]{2,1,0:T(8,128)(2,1)S(1)} collective-permute-done((bf16[64,16,128]{2,1,0:T(8,128)(2,1)S(1)}, bf16[64,16,128]{2,1,0:T(8,128)(2,1)S(1)}, u32[]{:S(2)}, u32[]{:S(2)}) %collective-permute-start.46) | collective-permute-done | bytes 262176 | tf_op jit(solution)/shard_map/ppermute | solution.py:289
  364.5 9.9 %collective-permute-done.47.refs_25_ = bf16[64,16,128]{2,1,0:T(8,128)(2,1)S(1)} collective-permute-done((bf16[64,16,128]{2,1,0:T(8,128)(2,1)S(1)}, bf16[64,16,128]{2,1,0:T(8,128)(2,1)S(1)}, u32[]{:S(2)}, u32[]{:S(2)}) %collective-permute-start.47) | collective-permute-done | bytes 262176 | tf_op jit(solution)/shard_map/ppermute | solution.py:289
  378.2 19.2 %collective-permute-start.33 = (bf16[64,16,128]{2,1,0:T(8,128)(2,1)S(1)}, bf16[64,16,128]{2,1,0:T(8,128)(2,1)S(1)}, u32[]{:S(2)}, u32[]{:S(2)}) collective-permute-start(bf16[64,16,128]{2,1,0:T(8,128)(2,1)S(1)} %get-tuple-element.174), channel_id=1, source_target_pairs={{0,1},{1,0},{2,3},{3,2},{4,5},{5,4},{6,7},{7,6},{8,9},{9,8},{10,11... | collective-permute-start | bytes 786440 | tf_op jit(solution)/shard_map/ppermute | solution.py:289
  405.4 20.1 %collective-permute-start.32 = (bf16[64,16,128]{2,1,0:T(8,128)(2,1)S(1)}, bf16[64,16,128]{2,1,0:T(8,128)(2,1)}, u32[]{:S(2)}, u32[]{:S(2)}) collective-permute-start(bf16[64,16,128]{2,1,0:T(8,128)(2,1)S(1)} %get-tuple-element.173), channel_id=1, source_target_pairs={{0,1},{1,0},{2,3},{3,2},{4,5},{5,4},{6,7},{7,6},{8,9},{9,8},{10,11... | collective-permute-start | bytes 786440 | tf_op jit(solution)/shard_map/ppermute | solution.py:289
  425.5 5.5 collective-permute-start.40
  436.6 10.9 %collective-permute-done.41.refs_19_ = bf16[64,16,128]{2,1,0:T(8,128)(2,1)S(1)} collective-permute-done((bf16[64,16,128]{2,1,0:T(8,128)(2,1)S(1)}, bf16[64,16,128]{2,1,0:T(8,128)(2,1)S(1)}, u32[]{:S(2)}, u32[]{:S(2)}) %collective-permute-start.41) | collective-permute-done | bytes 262176 | tf_op jit(solution)/shard_map/ppermute | solution.py:289
  447.5 11.3 %collective-permute-done.40.refs_18_ = bf16[64,16,128]{2,1,0:T(8,128)(2,1)} collective-permute-done((bf16[64,16,128]{2,1,0:T(8,128)(2,1)S(1)}, bf16[64,16,128]{2,1,0:T(8,128)(2,1)}, u32[]{:S(2)}, u32[]{:S(2)}) %collective-permute-start.40) | collective-permute-done | bytes 262176 | tf_op jit(solution)/shard_map/ppermute | solution.py:289
  458.9 16.9 %lines.1 = (bf16[64,16,128]{2,1,0:T(8,128)(2,1)S(1)}, bf16[64,16,128]{2,1,0:T(8,128)(2,1)S(1)}, bf16[64,16,128]{2,1,0:T(8,128)(2,1)S(1)}, bf16[64,16,128]{2,1,0:...) custom-call(s32[3]{0:T(128)S(1)} %pad_add_fusion.refs_0_, ...), custom_call_target="tpu_custom_call" | custom-call | flops 8589934592 | bytes 16777216 | tf_op jit(solution)/shard_map/lines/pallas_call | solution.py:216
  477.2 6.0 collective-permute-start.105
  487.3 7.6 collective-permute-done.105.refs_2_
  494.8 15.4 %collective-permute-done.106.refs_3_ = bf16[64,16,128]{2,1,0:T(8,128)(2,1)S(1)} collective-permute-done((bf16[64,16,128]{2,1,0:T(8,128)(2,1)S(1)}, bf16[64,16,128]{2,1,0:T(8,128)(2,1)S(1)}, u32[]{:S(2)}, u32[]{:S(2)}) %collective-permute-start.106) | collective-permute-done | bytes 262176 | tf_op jit(solution)/shard_map/ppermute | solution.py:289
  510.2 11.8 %collective-permute-start.92 = (bf16[64,16,128]{2,1,0:T(8,128)(2,1)S(1)}, bf16[64,16,128]{2,1,0:T(8,128)(2,1)S(1)}, u32[]{:S(2)}, u32[]{:S(2)}) collective-permute-start(bf16[64,16,128]{2,1,0:T(8,128)(2,1)S(1)} %get-tuple-element.239), channel_id=1, source_target_pairs={{0,2},{1,3},{2,0},{3,1},{4,6},{5,7},{6,4},{7,5},{8,10},{9,11},{10,... | collective-permute-start | bytes 786440 | tf_op jit(solution)/shard_map/ppermute | solution.py:289
  524.4 15.0 %collective-permute-start.84 = (bf16[64,16,128]{2,1,0:T(8,128)(2,1)S(1)}, bf16[64,16,128]{2,1,0:T(8,128)(2,1)S(1)}, u32[]{:S(2)}, u32[]{:S(2)}) collective-permute-start(bf16[64,16,128]{2,1,0:T(8,128)(2,1)S(1)} %get-tuple-element.230), channel_id=1, source_target_pairs={{0,1},{1,0},{2,3},{3,2},{4,5},{5,4},{6,7},{7,6},{8,9},{9,8},{10,11... | collective-permute-start | bytes 786440 | tf_op jit(solution)/shard_map/ppermute | solution.py:289
  545.4 15.4 %collective-permute-done.92.refs_3_ = bf16[64,16,128]{2,1,0:T(8,128)(2,1)S(1)} collective-permute-done((bf16[64,16,128]{2,1,0:T(8,128)(2,1)S(1)}, bf16[64,16,128]{2,1,0:T(8,128)(2,1)S(1)}, u32[]{:S(2)}, u32[]{:S(2)}) %collective-permute-start.92) | collective-permute-done | bytes 262176 | tf_op jit(solution)/shard_map/ppermute | solution.py:289
  560.8 6.1 collective-permute-start.78
  569.3 14.0 %collective-permute-done.85.refs_3_ = bf16[64,16,128]{2,1,0:T(8,128)(2,1)S(1)} collective-permute-done((bf16[64,16,128]{2,1,0:T(8,128)(2,1)S(1)}, bf16[64,16,128]{2,1,0:T(8,128)(2,1)S(1)}, u32[]{:S(2)}, u32[]{:S(2)}) %collective-permute-start.85) | collective-permute-done | bytes 262176 | tf_op jit(solution)/shard_map/ppermute | solution.py:289
  583.3 6.1 collective-permute-start.71
  591.9 14.0 %collective-permute-done.78.refs_3_ = bf16[64,16,128]{2,1,0:T(8,128)(2,1)S(1)} collective-permute-done((bf16[64,16,128]{2,1,0:T(8,128)(2,1)S(1)}, bf16[64,16,128]{2,1,0:T(8,128)(2,1)S(1)}, u32[]{:S(2)}, u32[]{:S(2)}) %collective-permute-start.78) | collective-permute-done | bytes 262176 | tf_op jit(solution)/shard_map/ppermute | solution.py:289
  605.8 6.1 collective-permute-start.64
  614.4 14.0 %collective-permute-done.71.refs_3_ = bf16[64,16,128]{2,1,0:T(8,128)(2,1)S(1)} collective-permute-done((bf16[64,16,128]{2,1,0:T(8,128)(2,1)S(1)}, bf16[64,16,128]{2,1,0:T(8,128)(2,1)S(1)}, u32[]{:S(2)}, u32[]{:S(2)}) %collective-permute-start.71) | collective-permute-done | bytes 262176 | tf_op jit(solution)/shard_map/ppermute | solution.py:289
  628.4 6.1 collective-permute-start.57
  639.3 11.6 %collective-permute-done.64.refs_3_ = bf16[64,16,128]{2,1,0:T(8,128)(2,1)S(1)} collective-permute-done((bf16[64,16,128]{2,1,0:T(8,128)(2,1)}, bf16[64,16,128]{2,1,0:T(8,128)(2,1)S(1)}, u32[]{:S(2)}, u32[]{:S(2)}) %collective-permute-start.64) | collective-permute-done | bytes 262176 | tf_op jit(solution)/shard_map/ppermute | solution.py:289
  655.1 7.0 collective-permute-done.57.refs_3_
  671.4 4.6 collective-permute-done.103.refs_4_
  682.5 4.7 collective-permute-done.96.refs_4_
  693.8 4.7 collective-permute-done.89.refs_4_
  730.1 4.8 collective-permute-done.68.refs_4_
  738.9 5.2 collective-permute-done.60.refs_3_
  759.4 16.6 %collective-permute-done.97.refs_6_ = bf16[16,256,128]{2,1,0:T(8,128)(2,1)S(1)} collective-permute-done((bf16[16,256,128]{2,1,0:T(8,128)(2,1)}, bf16[16,256,128]{2,1,0:T(8,128)(2,1)S(1)}, u32[]{:S(2)}, u32[]{:S(2)}) %collective-permute-start.97) | collective-permute-done | bytes 1048608 | tf_op jit(solution)/shard_map/ppermute | solution.py:289
  787.5 11.0 %collective-permute-done.90.refs_6_ = bf16[16,256,128]{2,1,0:T(8,128)(2,1)} collective-permute-done((bf16[16,256,128]{2,1,0:T(8,128)(2,1)}, bf16[16,256,128]{2,1,0:T(8,128)(2,1)}, u32[]{:S(2)}, u32[]{:S(2)}) %collective-permute-start.90) | collective-permute-done | bytes 1048608 | tf_op jit(solution)/shard_map/ppermute | solution.py:289
  801.6 19.3 %collective-permute-done.83.refs_6_ = bf16[16,256,128]{2,1,0:T(8,128)(2,1)S(1)} collective-permute-done((bf16[16,256,128]{2,1,0:T(8,128)(2,1)}, bf16[16,256,128]{2,1,0:T(8,128)(2,1)S(1)}, u32[]{:S(2)}, u32[]{:S(2)}) %collective-permute-start.83) | collective-permute-done | bytes 1048608 | tf_op jit(solution)/shard_map/ppermute | solution.py:289
  823.0 20.4 %collective-permute-done.76.refs_6_ = bf16[16,256,128]{2,1,0:T(8,128)(2,1)S(1)} collective-permute-done((bf16[16,256,128]{2,1,0:T(8,128)(2,1)}, bf16[16,256,128]{2,1,0:T(8,128)(2,1)S(1)}, u32[]{:S(2)}, u32[]{:S(2)}) %collective-permute-start.76) | collective-permute-done | bytes 1048608 | tf_op jit(solution)/shard_map/ppermute | solution.py:289
  845.4 20.4 %collective-permute-done.69.refs_6_ = bf16[16,256,128]{2,1,0:T(8,128)(2,1)S(1)} collective-permute-done((bf16[16,256,128]{2,1,0:T(8,128)(2,1)}, bf16[16,256,128]{2,1,0:T(8,128)(2,1)S(1)}, u32[]{:S(2)}, u32[]{:S(2)}) %collective-permute-start.69) | collective-permute-done | bytes 1048608 | tf_op jit(solution)/shard_map/ppermute | solution.py:289
  867.9 18.6 %collective-permute-done.62.refs_6_ = bf16[16,256,128]{2,1,0:T(8,128)(2,1)S(1)} collective-permute-done((bf16[16,256,128]{2,1,0:T(8,128)(2,1)}, bf16[16,256,128]{2,1,0:T(8,128)(2,1)S(1)}, u32[]{:S(2)}, u32[]{:S(2)}) %collective-permute-start.62) | collective-permute-done | bytes 1048608 | tf_op jit(solution)/shard_map/ppermute | solution.py:289
  (333 shorter events, 288.4 us)
Async XLA Ops:
  5.6 45.2 %collective-permute-start.12 = (bf16[16,256,128]{2,1,0:T(8,128)(2,1)S(1)}, bf16[16,256,128]{2,1,0:T(8,128)(2,1)S(1)}, u32[]{:S(2)}, u32[]{:S(2)}) collective-permute-start(bf16[16,256,128]{2,1,0:T(8,128)(2,1)S(1)} %copy_rows.11), channel_id=1, source_target_pairs={{0,16},{16,0},{1,17},{17,1},{2,18},{18,2},{3,19},{19,3},{4,20},{20... | collective-permute-start | bytes 3145736 | tf_op jit(solution)/shard_map/ppermute | solution.py:289
  6.9 66.3 %collective-permute-start.16 = (bf16[16,256,128]{2,1,0:T(8,128)(2,1)S(1)}, bf16[16,256,128]{2,1,0:T(8,128)(2,1)S(1)}, u32[]{:S(2)}, u32[]{:S(2)}) collective-permute-start(bf16[16,256,128]{2,1,0:T(8,128)(2,1)S(1)} %copy_rows.12), channel_id=1, source_target_pairs={{0,16},{16,0},{1,17},{17,1},{2,18},{18,2},{3,19},{19,3},{4,20},{20... | collective-permute-start | bytes 3145736 | tf_op jit(solution)/shard_map/ppermute | solution.py:289
  11.1 84.8 %collective-permute-start.20 = (bf16[16,256,128]{2,1,0:T(8,128)(2,1)}, bf16[16,256,128]{2,1,0:T(8,128)(2,1)}, u32[]{:S(2)}, u32[]{:S(2)}) collective-permute-start(bf16[16,256,128]{2,1,0:T(8,128)(2,1)} %copy_rows.13), channel_id=1, source_target_pairs={{0,16},{16,0},{1,17},{17,1},{2,18},{18,2},{3,19},{19,3},{4,20},{20... | collective-permute-start | bytes 3145736 | tf_op jit(solution)/shard_map/ppermute | solution.py:289
  13.2 105.1 %collective-permute-start.24 = (bf16[16,256,128]{2,1,0:T(8,128)(2,1)}, bf16[16,256,128]{2,1,0:T(8,128)(2,1)}, u32[]{:S(2)}, u32[]{:S(2)}) collective-permute-start(bf16[16,256,128]{2,1,0:T(8,128)(2,1)} %copy_rows.14), channel_id=1, source_target_pairs={{0,16},{16,0},{1,17},{17,1},{2,18},{18,2},{3,19},{19,3},{4,20},{20... | collective-permute-start | bytes 3145736 | tf_op jit(solution)/shard_map/ppermute | solution.py:289
  28.3 112.5 %collective-permute-start.28 = (bf16[16,256,128]{2,1,0:T(8,128)(2,1)}, bf16[16,256,128]{2,1,0:T(8,128)(2,1)}, u32[]{:S(2)}, u32[]{:S(2)}) collective-permute-start(bf16[16,256,128]{2,1,0:T(8,128)(2,1)} %copy_rows.15), channel_id=1, source_target_pairs={{0,16},{16,0},{1,17},{17,1},{2,18},{18,2},{3,19},{19,3},{4,20},{20... | collective-permute-start | bytes 3145736 | tf_op jit(solution)/shard_map/ppermute | solution.py:289
  50.8 112.4 %collective-permute-start.4 = (bf16[16,256,128]{2,1,0:T(8,128)(2,1)}, bf16[16,256,128]{2,1,0:T(8,128)(2,1)S(1)}, u32[]{:S(2)}, u32[]{:S(2)}) collective-permute-start(bf16[16,256,128]{2,1,0:T(8,128)(2,1)} %copy_rows.9), channel_id=1, source_target_pairs={{0,16},{16,0},{1,17},{17,1},{2,18},{18,2},{3,19},{19,3},{4,20},{20... | collective-permute-start | bytes 3145736 | tf_op jit(solution)/shard_map/ppermute | solution.py:289
  74.2 110.5 %collective-permute-start = (bf16[16,256,128]{2,1,0:T(8,128)(2,1)}, bf16[16,256,128]{2,1,0:T(8,128)(2,1)S(1)}, u32[]{:S(2)}, u32[]{:S(2)}) collective-permute-start(bf16[16,256,128]{2,1,0:T(8,128)(2,1)} %copy_rows.8), channel_id=1, source_target_pairs={{0,16},{16,0},{1,17},{17,1},{2,18},{18,2},{3,19},{19,3},{4,20},{20... | collective-permute-start | bytes 3145736 | tf_op jit(solution)/shard_map/ppermute | solution.py:289
  95.9 90.6 %collective-permute-start.10 = (bf16[16,64,128]{2,1,0:T(8,128)(2,1)S(1)}, bf16[16,64,128]{2,1,0:T(8,128)(2,1)S(1)}, u32[]{:S(2)}, u32[]{:S(2)}) collective-permute-start(bf16[16,64,128]{2,1,0:T(8,128)(2,1)S(1)} %get-tuple-element.145), channel_id=1, source_target_pairs={{0,8},{4,12},{8,0},{12,4},{1,9},{5,13},{9,1},{13,5},{2,10},{6,14},... | collective-permute-start | bytes 786440 | tf_op jit(solution)/shard_map/ppermute | solution.py:289
  118.3 68.2 %collective-permute-start.11 = (bf16[16,64,128]{2,1,0:T(8,128)(2,1)S(1)}, bf16[16,64,128]{2,1,0:T(8,128)(2,1)S(1)}, u32[]{:S(2)}, u32[]{:S(2)}) collective-permute-start(bf16[16,64,128]{2,1,0:T(8,128)(2,1)S(1)} %get-tuple-element.146), channel_id=1, source_target_pairs={{0,12},{4,8},{8,4},{12,0},{1,13},{5,9},{9,5},{13,1},{2,14},{6,10},... | collective-permute-start | bytes 786440 | tf_op jit(solution)/shard_map/ppermute | solution.py:289
  140.8 46.1 %collective-permute-start.9 = (bf16[16,64,128]{2,1,0:T(8,128)(2,1)S(1)}, bf16[16,64,128]{2,1,0:T(8,128)(2,1)S(1)}, u32[]{:S(2)}, u32[]{:S(2)}) collective-permute-start(bf16[16,64,128]{2,1,0:T(8,128)(2,1)S(1)} %get-tuple-element.144), channel_id=1, source_target_pairs={{0,4},{4,0},{8,12},{12,8},{1,5},{5,1},{9,13},{13,9},{2,6},{6,2},{1... | collective-permute-start | bytes 786440 | tf_op jit(solution)/shard_map/ppermute | solution.py:289
  268.1 37.0 %collective-permute-start.39 = (bf16[64,16,128]{2,1,0:T(8,128)(2,1)S(1)}, bf16[64,16,128]{2,1,0:T(8,128)(2,1)S(1)}, u32[]{:S(2)}, u32[]{:S(2)}) collective-permute-start(bf16[64,16,128]{2,1,0:T(8,128)(2,1)S(1)} %get-tuple-element.180), channel_id=1, source_target_pairs={{0,1},{1,0},{2,3},{3,2},{4,5},{5,4},{6,7},{7,6},{8,9},{9,8},{10,11... | collective-permute-start | bytes 786440 | tf_op jit(solution)/shard_map/ppermute | solution.py:289
  271.9 34.7 %collective-permute-start.42 = (bf16[64,16,128]{2,1,0:T(8,128)(2,1)S(1)}, bf16[64,16,128]{2,1,0:T(8,128)(2,1)S(1)}, u32[]{:S(2)}, u32[]{:S(2)}) collective-permute-start(bf16[64,16,128]{2,1,0:T(8,128)(2,1)S(1)} %get-tuple-element.183), channel_id=1, source_target_pairs={{0,2},{1,3},{2,0},{3,1},{4,6},{5,7},{6,4},{7,5},{8,10},{9,11},{10,... | collective-permute-start | bytes 786440 | tf_op jit(solution)/shard_map/ppermute | solution.py:289
  294.4 46.3 %collective-permute-start.44 = (bf16[64,16,128]{2,1,0:T(8,128)(2,1)S(1)}, bf16[64,16,128]{2,1,0:T(8,128)(2,1)S(1)}, u32[]{:S(2)}, u32[]{:S(2)}) collective-permute-start(bf16[64,16,128]{2,1,0:T(8,128)(2,1)S(1)} %get-tuple-element.185), channel_id=1, source_target_pairs={{0,2},{1,3},{2,0},{3,1},{4,6},{5,7},{6,4},{7,5},{8,10},{9,11},{10,... | collective-permute-start | bytes 786440 | tf_op jit(solution)/shard_map/ppermute | solution.py:289
  300.2 51.7 %collective-permute-start.45 = (bf16[64,16,128]{2,1,0:T(8,128)(2,1)S(1)}, bf16[64,16,128]{2,1,0:T(8,128)(2,1)S(1)}, u32[]{:S(2)}, u32[]{:S(2)}) collective-permute-start(bf16[64,16,128]{2,1,0:T(8,128)(2,1)S(1)} %get-tuple-element.186), channel_id=1, source_target_pairs={{0,2},{1,3},{2,0},{3,1},{4,6},{5,7},{6,4},{7,5},{8,10},{9,11},{10,... | collective-permute-start | bytes 786440 | tf_op jit(solution)/shard_map/ppermute | solution.py:289
  305.1 58.1 %collective-permute-start.46 = (bf16[64,16,128]{2,1,0:T(8,128)(2,1)S(1)}, bf16[64,16,128]{2,1,0:T(8,128)(2,1)S(1)}, u32[]{:S(2)}, u32[]{:S(2)}) collective-permute-start(bf16[64,16,128]{2,1,0:T(8,128)(2,1)S(1)} %get-tuple-element.187), channel_id=1, source_target_pairs={{0,2},{1,3},{2,0},{3,1},{4,6},{5,7},{6,4},{7,5},{8,10},{9,11},{10,... | collective-permute-start | bytes 786440 | tf_op jit(solution)/shard_map/ppermute | solution.py:289
  306.7 67.7 %collective-permute-start.47 = (bf16[64,16,128]{2,1,0:T(8,128)(2,1)S(1)}, bf16[64,16,128]{2,1,0:T(8,128)(2,1)S(1)}, u32[]{:S(2)}, u32[]{:S(2)}) collective-permute-start(bf16[64,16,128]{2,1,0:T(8,128)(2,1)S(1)} %get-tuple-element.188), channel_id=1, source_target_pairs={{0,2},{1,3},{2,0},{3,1},{4,6},{5,7},{6,4},{7,5},{8,10},{9,11},{10,... | collective-permute-start | bytes 786440 | tf_op jit(solution)/shard_map/ppermute | solution.py:289
  308.0 67.8 %collective-permute-start.50 = (bf16[64,16,128]{2,1,0:T(8,128)(2,1)S(1)}, bf16[64,16,128]{2,1,0:T(8,128)(2,1)S(1)}, u32[]{:S(2)}, u32[]{:S(2)}) collective-permute-start(bf16[64,16,128]{2,1,0:T(8,128)(2,1)S(1)} %get-tuple-element.191), channel_id=1, source_target_pairs={{0,3},{1,2},{2,1},{3,0},{4,7},{5,6},{6,5},{7,4},{8,11},{9,10},{10,... | collective-permute-start | bytes 786440 | tf_op jit(solution)/shard_map/ppermute | solution.py:289
  340.7 37.5 %collective-permute-start.51 = (bf16[64,16,128]{2,1,0:T(8,128)(2,1)S(1)}, bf16[64,16,128]{2,1,0:T(8,128)(2,1)S(1)}, u32[]{:S(2)}, u32[]{:S(2)}) collective-permute-start(bf16[64,16,128]{2,1,0:T(8,128)(2,1)S(1)} %get-tuple-element.192), channel_id=1, source_target_pairs={{0,3},{1,2},{2,1},{3,0},{4,7},{5,6},{6,5},{7,4},{8,11},{9,10},{10,... | collective-permute-start | bytes 786440 | tf_op jit(solution)/shard_map/ppermute | solution.py:289
  351.9 48.7 %collective-permute-start.52 = (bf16[64,16,128]{2,1,0:T(8,128)(2,1)S(1)}, bf16[64,16,128]{2,1,0:T(8,128)(2,1)S(1)}, u32[]{:S(2)}, u32[]{:S(2)}) collective-permute-start(bf16[64,16,128]{2,1,0:T(8,128)(2,1)S(1)} %get-tuple-element.193), channel_id=1, source_target_pairs={{0,3},{1,2},{2,1},{3,0},{4,7},{5,6},{6,5},{7,4},{8,11},{9,10},{10,... | collective-permute-start | bytes 786440 | tf_op jit(solution)/shard_map/ppermute | solution.py:289
  363.2 39.8 %collective-permute-start.53 = (bf16[64,16,128]{2,1,0:T(8,128)(2,1)S(1)}, bf16[64,16,128]{2,1,0:T(8,128)(2,1)S(1)}, u32[]{:S(2)}, u32[]{:S(2)}) collective-permute-start(bf16[64,16,128]{2,1,0:T(8,128)(2,1)S(1)} %get-tuple-element.194), channel_id=1, source_target_pairs={{0,3},{1,2},{2,1},{3,0},{4,7},{5,6},{6,5},{7,4},{8,11},{9,10},{10,... | collective-permute-start | bytes 786440 | tf_op jit(solution)/shard_map/ppermute | solution.py:289
  375.8 49.8 %collective-permute-start.55 = (bf16[64,16,128]{2,1,0:T(8,128)(2,1)S(1)}, bf16[64,16,128]{2,1,0:T(8,128)(2,1)S(1)}, u32[]{:S(2)}, u32[]{:S(2)}) collective-permute-start(bf16[64,16,128]{2,1,0:T(8,128)(2,1)S(1)} %get-tuple-element.196), channel_id=1, source_target_pairs={{0,3},{1,2},{2,1},{3,0},{4,7},{5,6},{6,5},{7,4},{8,11},{9,10},{10,... | collective-permute-start | bytes 786440 | tf_op jit(solution)/shard_map/ppermute | solution.py:289
  378.2 52.8 %collective-permute-start.33 = (bf16[64,16,128]{2,1,0:T(8,128)(2,1)S(1)}, bf16[64,16,128]{2,1,0:T(8,128)(2,1)S(1)}, u32[]{:S(2)}, u32[]{:S(2)}) collective-permute-start(bf16[64,16,128]{2,1,0:T(8,128)(2,1)S(1)} %get-tuple-element.174), channel_id=1, source_target_pairs={{0,1},{1,0},{2,3},{3,2},{4,5},{5,4},{6,7},{7,6},{8,9},{9,8},{10,11... | collective-permute-start | bytes 786440 | tf_op jit(solution)/shard_map/ppermute | solution.py:289
  400.7 46.8 %collective-permute-start.41 = (bf16[64,16,128]{2,1,0:T(8,128)(2,1)S(1)}, bf16[64,16,128]{2,1,0:T(8,128)(2,1)S(1)}, u32[]{:S(2)}, u32[]{:S(2)}) collective-permute-start(bf16[64,16,128]{2,1,0:T(8,128)(2,1)S(1)} %get-tuple-element.182), channel_id=1, source_target_pairs={{0,2},{1,3},{2,0},{3,1},{4,6},{5,7},{6,4},{7,5},{8,10},{9,11},{10,... | collective-permute-start | bytes 786440 | tf_op jit(solution)/shard_map/ppermute | solution.py:289
  403.0 44.5 %collective-permute-start.49 = (bf16[64,16,128]{2,1,0:T(8,128)(2,1)S(1)}, bf16[64,16,128]{2,1,0:T(8,128)(2,1)S(1)}, u32[]{:S(2)}, u32[]{:S(2)}) collective-permute-start(bf16[64,16,128]{2,1,0:T(8,128)(2,1)S(1)} %get-tuple-element.190), channel_id=1, source_target_pairs={{0,3},{1,2},{2,1},{3,0},{4,7},{5,6},{6,5},{7,4},{8,11},{9,10},{10,... | collective-permute-start | bytes 786440 | tf_op jit(solution)/shard_map/ppermute | solution.py:289
  405.4 42.1 %collective-permute-start.32 = (bf16[64,16,128]{2,1,0:T(8,128)(2,1)S(1)}, bf16[64,16,128]{2,1,0:T(8,128)(2,1)}, u32[]{:S(2)}, u32[]{:S(2)}) collective-permute-start(bf16[64,16,128]{2,1,0:T(8,128)(2,1)S(1)} %get-tuple-element.173), channel_id=1, source_target_pairs={{0,1},{1,0},{2,3},{3,2},{4,5},{5,4},{6,7},{7,6},{8,9},{9,8},{10,11... | collective-permute-start | bytes 786440 | tf_op jit(solution)/shard_map/ppermute | solution.py:289
  485.6 36.4 %collective-permute-start.100 = (bf16[64,16,128]{2,1,0:T(8,128)(2,1)}, bf16[64,16,128]{2,1,0:T(8,128)(2,1)S(1)}, u32[]{:S(2)}, u32[]{:S(2)}) collective-permute-start(bf16[64,16,128]{2,1,0:T(8,128)(2,1)} %get-tuple-element.248), channel_id=1, source_target_pairs={{0,3},{1,2},{2,1},{3,0},{4,7},{5,6},{6,5},{7,4},{8,11},{9,10},{10,... | collective-permute-start | bytes 786440 | tf_op jit(solution)/shard_map/ppermute | solution.py:289
  487.0 37.3 %collective-permute-start.98 = (bf16[64,16,128]{2,1,0:T(8,128)(2,1)S(1)}, bf16[64,16,128]{2,1,0:T(8,128)(2,1)S(1)}, u32[]{:S(2)}, u32[]{:S(2)}) collective-permute-start(bf16[64,16,128]{2,1,0:T(8,128)(2,1)S(1)} %get-tuple-element.246), channel_id=1, source_target_pairs={{0,1},{1,0},{2,3},{3,2},{4,5},{5,4},{6,7},{7,6},{8,9},{9,8},{10,11... | collective-permute-start | bytes 786440 | tf_op jit(solution)/shard_map/ppermute | solution.py:289
  494.8 49.2 %collective-permute-start.99 = (bf16[64,16,128]{2,1,0:T(8,128)(2,1)S(1)}, bf16[64,16,128]{2,1,0:T(8,128)(2,1)S(1)}, u32[]{:S(2)}, u32[]{:S(2)}) collective-permute-start(bf16[64,16,128]{2,1,0:T(8,128)(2,1)S(1)} %get-tuple-element.247), channel_id=1, source_target_pairs={{0,2},{1,3},{2,0},{3,1},{4,6},{5,7},{6,4},{7,5},{8,10},{9,11},{10,... | collective-permute-start | bytes 786440 | tf_op jit(solution)/shard_map/ppermute | solution.py:289
  510.2 33.8 %collective-permute-start.91 = (bf16[64,16,128]{2,1,0:T(8,128)(2,1)S(1)}, bf16[64,16,128]{2,1,0:T(8,128)(2,1)S(1)}, u32[]{:S(2)}, u32[]{:S(2)}) collective-permute-start(bf16[64,16,128]{2,1,0:T(8,128)(2,1)S(1)} %get-tuple-element.238), channel_id=1, source_target_pairs={{0,1},{1,0},{2,3},{3,2},{4,5},{5,4},{6,7},{7,6},{8,9},{9,8},{10,11... | collective-permute-start | bytes 786440 | tf_op jit(solution)/shard_map/ppermute | solution.py:289
  510.2 50.6 %collective-permute-start.92 = (bf16[64,16,128]{2,1,0:T(8,128)(2,1)S(1)}, bf16[64,16,128]{2,1,0:T(8,128)(2,1)S(1)}, u32[]{:S(2)}, u32[]{:S(2)}) collective-permute-start(bf16[64,16,128]{2,1,0:T(8,128)(2,1)S(1)} %get-tuple-element.239), channel_id=1, source_target_pairs={{0,2},{1,3},{2,0},{3,1},{4,6},{5,7},{6,4},{7,5},{8,10},{9,11},{10,... | collective-permute-start | bytes 786440 | tf_op jit(solution)/shard_map/ppermute | solution.py:289
  522.0 38.8 %collective-permute-start.93 = (bf16[64,16,128]{2,1,0:T(8,128)(2,1)}, bf16[64,16,128]{2,1,0:T(8,128)(2,1)S(1)}, u32[]{:S(2)}, u32[]{:S(2)}) collective-permute-start(bf16[64,16,128]{2,1,0:T(8,128)(2,1)} %get-tuple-element.240), channel_id=1, source_target_pairs={{0,3},{1,2},{2,1},{3,0},{4,7},{5,6},{6,5},{7,4},{8,11},{9,10},{10,... | collective-permute-start | bytes 786440 | tf_op jit(solution)/shard_map/ppermute | solution.py:289
  524.4 42.6 %collective-permute-start.84 = (bf16[64,16,128]{2,1,0:T(8,128)(2,1)S(1)}, bf16[64,16,128]{2,1,0:T(8,128)(2,1)S(1)}, u32[]{:S(2)}, u32[]{:S(2)}) collective-permute-start(bf16[64,16,128]{2,1,0:T(8,128)(2,1)S(1)} %get-tuple-element.230), channel_id=1, source_target_pairs={{0,1},{1,0},{2,3},{3,2},{4,5},{5,4},{6,7},{7,6},{8,9},{9,8},{10,11... | collective-permute-start | bytes 786440 | tf_op jit(solution)/shard_map/ppermute | solution.py:289
  544.0 39.3 %collective-permute-start.85 = (bf16[64,16,128]{2,1,0:T(8,128)(2,1)S(1)}, bf16[64,16,128]{2,1,0:T(8,128)(2,1)S(1)}, u32[]{:S(2)}, u32[]{:S(2)}) collective-permute-start(bf16[64,16,128]{2,1,0:T(8,128)(2,1)S(1)} %get-tuple-element.231), channel_id=1, source_target_pairs={{0,2},{1,3},{2,0},{3,1},{4,6},{5,7},{6,4},{7,5},{8,10},{9,11},{10,... | collective-permute-start | bytes 786440 | tf_op jit(solution)/shard_map/ppermute | solution.py:289
  544.0 39.3 %collective-permute-start.86 = (bf16[64,16,128]{2,1,0:T(8,128)(2,1)}, bf16[64,16,128]{2,1,0:T(8,128)(2,1)S(1)}, u32[]{:S(2)}, u32[]{:S(2)}) collective-permute-start(bf16[64,16,128]{2,1,0:T(8,128)(2,1)} %get-tuple-element.232), channel_id=1, source_target_pairs={{0,3},{1,2},{2,1},{3,0},{4,7},{5,6},{6,5},{7,4},{8,11},{9,10},{10,... | collective-permute-start | bytes 786440 | tf_op jit(solution)/shard_map/ppermute | solution.py:289
  560.8 45.0 %collective-permute-start.78 = (bf16[64,16,128]{2,1,0:T(8,128)(2,1)S(1)}, bf16[64,16,128]{2,1,0:T(8,128)(2,1)S(1)}, u32[]{:S(2)}, u32[]{:S(2)}) collective-permute-start(bf16[64,16,128]{2,1,0:T(8,128)(2,1)S(1)} %get-tuple-element.223), channel_id=1, source_target_pairs={{0,2},{1,3},{2,0},{3,1},{4,6},{5,7},{6,4},{7,5},{8,10},{9,11},{10,... | collective-permute-start | bytes 786440 | tf_op jit(solution)/shard_map/ppermute | solution.py:289
  567.0 38.9 %collective-permute-start.79 = (bf16[64,16,128]{2,1,0:T(8,128)(2,1)}, bf16[64,16,128]{2,1,0:T(8,128)(2,1)S(1)}, u32[]{:S(2)}, u32[]{:S(2)}) collective-permute-start(bf16[64,16,128]{2,1,0:T(8,128)(2,1)} %get-tuple-element.224), channel_id=1, source_target_pairs={{0,3},{1,2},{2,1},{3,0},{4,7},{5,6},{6,5},{7,4},{8,11},{9,10},{10,... | collective-permute-start | bytes 786440 | tf_op jit(solution)/shard_map/ppermute | solution.py:289
  583.3 45.0 %collective-permute-start.71 = (bf16[64,16,128]{2,1,0:T(8,128)(2,1)S(1)}, bf16[64,16,128]{2,1,0:T(8,128)(2,1)S(1)}, u32[]{:S(2)}, u32[]{:S(2)}) collective-permute-start(bf16[64,16,128]{2,1,0:T(8,128)(2,1)S(1)} %get-tuple-element.215), channel_id=1, source_target_pairs={{0,2},{1,3},{2,0},{3,1},{4,6},{5,7},{6,4},{7,5},{8,10},{9,11},{10,... | collective-permute-start | bytes 786440 | tf_op jit(solution)/shard_map/ppermute | solution.py:289
  589.5 38.9 %collective-permute-start.72 = (bf16[64,16,128]{2,1,0:T(8,128)(2,1)}, bf16[64,16,128]{2,1,0:T(8,128)(2,1)S(1)}, u32[]{:S(2)}, u32[]{:S(2)}) collective-permute-start(bf16[64,16,128]{2,1,0:T(8,128)(2,1)} %get-tuple-element.216), channel_id=1, source_target_pairs={{0,3},{1,2},{2,1},{3,0},{4,7},{5,6},{6,5},{7,4},{8,11},{9,10},{10,... | collective-permute-start | bytes 786440 | tf_op jit(solution)/shard_map/ppermute | solution.py:289
  605.8 45.0 %collective-permute-start.64 = (bf16[64,16,128]{2,1,0:T(8,128)(2,1)}, bf16[64,16,128]{2,1,0:T(8,128)(2,1)S(1)}, u32[]{:S(2)}, u32[]{:S(2)}) collective-permute-start(bf16[64,16,128]{2,1,0:T(8,128)(2,1)} %get-tuple-element.207), channel_id=1, source_target_pairs={{0,2},{1,3},{2,0},{3,1},{4,6},{5,7},{6,4},{7,5},{8,10},{9,11},{10,... | collective-permute-start | bytes 786440 | tf_op jit(solution)/shard_map/ppermute | solution.py:289
  612.0 38.9 %collective-permute-start.65 = (bf16[64,16,128]{2,1,0:T(8,128)(2,1)}, bf16[64,16,128]{2,1,0:T(8,128)(2,1)S(1)}, u32[]{:S(2)}, u32[]{:S(2)}) collective-permute-start(bf16[64,16,128]{2,1,0:T(8,128)(2,1)} %get-tuple-element.208), channel_id=1, source_target_pairs={{0,3},{1,2},{2,1},{3,0},{4,7},{5,6},{6,5},{7,4},{8,11},{9,10},{10,... | collective-permute-start | bytes 786440 | tf_op jit(solution)/shard_map/ppermute | solution.py:289
  705.0 47.2 %collective-permute-start.111 = (bf16[16,256,128]{2,1,0:T(8,128)(2,1)S(1)}, bf16[16,256,128]{2,1,0:T(8,128)(2,1)S(1)}, u32[]{:S(2)}, u32[]{:S(2)}) collective-permute-start(bf16[16,256,128]{2,1,0:T(8,128)(2,1)S(1)} %inverse_y.23), channel_id=1, source_target_pairs={{0,16},{16,0},{1,17},{17,1},{2,18},{18,2},{3,19},{19,3},{4,20},{20... | collective-permute-start | bytes 3145736 | tf_op jit(solution)/shard_map/ppermute | solution.py:289
  709.7 46.3 %collective-permute-start.104 = (bf16[16,256,128]{2,1,0:T(8,128)(2,1)S(1)}, bf16[16,256,128]{2,1,0:T(8,128)(2,1)S(1)}, u32[]{:S(2)}, u32[]{:S(2)}) collective-permute-start(bf16[16,256,128]{2,1,0:T(8,128)(2,1)S(1)} %inverse_y.22), channel_id=1, source_target_pairs={{0,16},{16,0},{1,17},{17,1},{2,18},{18,2},{3,19},{19,3},{4,20},{20... | collective-permute-start | bytes 3145736 | tf_op jit(solution)/shard_map/ppermute | solution.py:289
  713.0 62.9 %collective-permute-start.97 = (bf16[16,256,128]{2,1,0:T(8,128)(2,1)}, bf16[16,256,128]{2,1,0:T(8,128)(2,1)S(1)}, u32[]{:S(2)}, u32[]{:S(2)}) collective-permute-start(bf16[16,256,128]{2,1,0:T(8,128)(2,1)} %inverse_y.21), channel_id=1, source_target_pairs={{0,16},{16,0},{1,17},{17,1},{2,18},{18,2},{3,19},{19,3},{4,20},{20... | collective-permute-start | bytes 3145736 | tf_op jit(solution)/shard_map/ppermute | solution.py:289
  744.1 54.4 %collective-permute-start.90 = (bf16[16,256,128]{2,1,0:T(8,128)(2,1)}, bf16[16,256,128]{2,1,0:T(8,128)(2,1)}, u32[]{:S(2)}, u32[]{:S(2)}) collective-permute-start(bf16[16,256,128]{2,1,0:T(8,128)(2,1)} %inverse_y.20), channel_id=1, source_target_pairs={{0,16},{16,0},{1,17},{17,1},{2,18},{18,2},{3,19},{19,3},{4,20},{20... | collective-permute-start | bytes 3145736 | tf_op jit(solution)/shard_map/ppermute | solution.py:289
  748.8 72.1 %collective-permute-start.83 = (bf16[16,256,128]{2,1,0:T(8,128)(2,1)}, bf16[16,256,128]{2,1,0:T(8,128)(2,1)S(1)}, u32[]{:S(2)}, u32[]{:S(2)}) collective-permute-start(bf16[16,256,128]{2,1,0:T(8,128)(2,1)} %inverse_y.19), channel_id=1, source_target_pairs={{0,16},{16,0},{1,17},{17,1},{2,18},{18,2},{3,19},{19,3},{4,20},{20... | collective-permute-start | bytes 3145736 | tf_op jit(solution)/shard_map/ppermute | solution.py:289
  753.1 90.3 %collective-permute-start.76 = (bf16[16,256,128]{2,1,0:T(8,128)(2,1)}, bf16[16,256,128]{2,1,0:T(8,128)(2,1)S(1)}, u32[]{:S(2)}, u32[]{:S(2)}) collective-permute-start(bf16[16,256,128]{2,1,0:T(8,128)(2,1)} %inverse_y.18), channel_id=1, source_target_pairs={{0,16},{16,0},{1,17},{17,1},{2,18},{18,2},{3,19},{19,3},{4,20},{20... | collective-permute-start | bytes 3145736 | tf_op jit(solution)/shard_map/ppermute | solution.py:289
  756.0 109.8 %collective-permute-start.69 = (bf16[16,256,128]{2,1,0:T(8,128)(2,1)}, bf16[16,256,128]{2,1,0:T(8,128)(2,1)S(1)}, u32[]{:S(2)}, u32[]{:S(2)}) collective-permute-start(bf16[16,256,128]{2,1,0:T(8,128)(2,1)} %inverse_y.17), channel_id=1, source_target_pairs={{0,16},{16,0},{1,17},{17,1},{2,18},{18,2},{3,19},{19,3},{4,20},{20... | collective-permute-start | bytes 3145736 | tf_op jit(solution)/shard_map/ppermute | solution.py:289
  776.0 110.6 %collective-permute-start.62 = (bf16[16,256,128]{2,1,0:T(8,128)(2,1)}, bf16[16,256,128]{2,1,0:T(8,128)(2,1)S(1)}, u32[]{:S(2)}, u32[]{:S(2)}) collective-permute-start(bf16[16,256,128]{2,1,0:T(8,128)(2,1)} %inverse_y.16), channel_id=1, source_target_pairs={{0,16},{16,0},{1,17},{17,1},{2,18},{18,2},{3,19},{19,3},{4,20},{20... | collective-permute-start | bytes 3145736 | tf_op jit(solution)/shard_map/ppermute | solution.py:289
  (116 other events, 4352.1 us)

commit v2 on v1

--- a/solution.py
+++ b/solution.py
@@ -57,8 +57,8 @@
     steps = [f"W{c}" for c in range(AHEAD["W"])]
     for c in range(n):
         steps += [f"B{c}", f"H{c}"] + [f"W{c + AHEAD['W']}"] * (c + AHEAD["W"] < n)
-        steps += [f"P{c}", f"T{c}"] + [f"R{c - 2}"] * (c > 1)
-    return steps + [f"R{n - 2}", f"R{n - 1}"]
+        steps += [f"R{c - 3}"] * (c > 2) + [f"P{c}", f"T{c}"]
+    return steps + [f"R{c}" for c in range(n - 3, n)]
 
 
 def partners(count):
@@ -209,7 +209,7 @@
 def lines(place, pieces, forward, inverse, base, lam_y, parts, sizes):
     q, _, cols = pieces[0].shape
     depth = forward.shape[0]
-    step = 8
+    step = 16
     spec = lambda n: pl.BlockSpec((step, n, cols), lambda i, s, t: (i, 0, 0))
     whole = lambda x: pl.BlockSpec(x.shape, lambda i, s, t: (0, 0))
     outs = [n for _ in range(parts) for n in sizes]

time: 889 us -> 887 us (level)
  no operation moved by 1% of the time
where the time goes in v2:
time: 887 us; the launch traced here: 886 us
  waiting for transfers between devices  537 us (61%)
  starting transfers between devices  212 us (24%)
  Pallas kernels  121 us (14%)
  local copies, waits for them, and re-layouts  14.9 us (2%)
    ppermute x112, waiting for transfers between devices, swap(): return lax.ppermute(value, axis, [(i, i ^ k) for i in range(count)])  537 us
    ppermute x112, starting transfers between devices, swap(): return lax.ppermute(value, axis, [(i, i ^ k) for i in range(count)])  212 us
    pallas_call x16, Pallas kernels, along_x(): pl.pallas_call(functools.partial(along_x_kernel, count=len(pieces), outs=...  39.5 us
    pallas_call x16, Pallas kernels, inverse_y(): pl.pallas_call(functools.partial(inverse_y_kernel, count=count, adds=len(...  32.6 us
    pallas_call x8, Pallas kernels, forward_y(): pl.pallas_call(functools.partial(forward_y_kernel, count=count, outs=outs...  20.6 us
  transfers between devices with their start and end apart: 112, of which 55 were waited for; matrix products, arithmetic and copies ran while one was open for 0% of the time, Pallas kernels for 12%

profile of v2, /device:TPU:0, one launch (start us, length us, event | category | flops | bytes accessed | tf_op | source)
XLA Modules:
  0.0 886.4 jit_solution(16144308371556035188)
XLA Ops:
  17.2 11.1 %collective-permute-done.8.refs_2_ = bf16[16,256,128]{2,1,0:T(8,128)(2,1)S(1)} collective-permute-done((bf16[16,256,128]{2,1,0:T(8,128)(2,1)S(1)}, bf16[16,256,128]{2,1,0:T(8,128)(2,1)S(1)}, u32[]{:S(2)}, u32[]{:S(2)}) %collective-permute-start.8) | collective-permute-done | bytes 1048608 | tf_op jit(solution)/shard_map/ppermute | solution.py:289
  32.5 18.3 %collective-permute-done.12.refs_2_ = bf16[16,256,128]{2,1,0:T(8,128)(2,1)S(1)} collective-permute-done((bf16[16,256,128]{2,1,0:T(8,128)(2,1)S(1)}, bf16[16,256,128]{2,1,0:T(8,128)(2,1)S(1)}, u32[]{:S(2)}, u32[]{:S(2)}) %collective-permute-start.12) | collective-permute-done | bytes 1048608 | tf_op jit(solution)/shard_map/ppermute | solution.py:289
  54.9 18.4 %collective-permute-done.16.refs_2_ = bf16[16,256,128]{2,1,0:T(8,128)(2,1)S(1)} collective-permute-done((bf16[16,256,128]{2,1,0:T(8,128)(2,1)S(1)}, bf16[16,256,128]{2,1,0:T(8,128)(2,1)S(1)}, u32[]{:S(2)}, u32[]{:S(2)}) %collective-permute-start.16) | collective-permute-done | bytes 1048608 | tf_op jit(solution)/shard_map/ppermute | solution.py:289
  80.2 15.7 %collective-permute-done.20.refs_2_ = bf16[16,256,128]{2,1,0:T(8,128)(2,1)} collective-permute-done((bf16[16,256,128]{2,1,0:T(8,128)(2,1)}, bf16[16,256,128]{2,1,0:T(8,128)(2,1)}, u32[]{:S(2)}, u32[]{:S(2)}) %collective-permute-start.20) | collective-permute-done | bytes 1048608 | tf_op jit(solution)/shard_map/ppermute | solution.py:289
  97.8 20.5 %collective-permute-done.24.refs_2_ = bf16[16,256,128]{2,1,0:T(8,128)(2,1)} collective-permute-done((bf16[16,256,128]{2,1,0:T(8,128)(2,1)}, bf16[16,256,128]{2,1,0:T(8,128)(2,1)}, u32[]{:S(2)}, u32[]{:S(2)}) %collective-permute-start.24) | collective-permute-done | bytes 1048608 | tf_op jit(solution)/shard_map/ppermute | solution.py:289
  118.3 22.5 %collective-permute-done.28.refs_2_ = bf16[16,256,128]{2,1,0:T(8,128)(2,1)} collective-permute-done((bf16[16,256,128]{2,1,0:T(8,128)(2,1)}, bf16[16,256,128]{2,1,0:T(8,128)(2,1)}, u32[]{:S(2)}, u32[]{:S(2)}) %collective-permute-start.28) | collective-permute-done | bytes 1048608 | tf_op jit(solution)/shard_map/ppermute | solution.py:289
  145.8 17.3 %collective-permute-done.4.refs_2_ = bf16[16,256,128]{2,1,0:T(8,128)(2,1)S(1)} collective-permute-done((bf16[16,256,128]{2,1,0:T(8,128)(2,1)}, bf16[16,256,128]{2,1,0:T(8,128)(2,1)S(1)}, u32[]{:S(2)}, u32[]{:S(2)}) %collective-permute-start.4) | collective-permute-done | bytes 1048608 | tf_op jit(solution)/shard_map/ppermute | solution.py:289
  163.2 21.6 %collective-permute-done.refs_2_ = bf16[16,256,128]{2,1,0:T(8,128)(2,1)S(1)} collective-permute-done((bf16[16,256,128]{2,1,0:T(8,128)(2,1)}, bf16[16,256,128]{2,1,0:T(8,128)(2,1)S(1)}, u32[]{:S(2)}, u32[]{:S(2)}) %collective-permute-start) | collective-permute-done | bytes 1048608 | tf_op jit(solution)/shard_map/ppermute | solution.py:289
  216.4 4.8 collective-permute-done.23.refs_4_
  238.9 4.8 collective-permute-done.31.refs_4_
  274.8 8.4 collective-permute-done.36.refs_14_
  285.1 9.3 %collective-permute-done.37.refs_15_ = bf16[64,16,128]{2,1,0:T(8,128)(2,1)S(1)} collective-permute-done((bf16[64,16,128]{2,1,0:T(8,128)(2,1)S(1)}, bf16[64,16,128]{2,1,0:T(8,128)(2,1)S(1)}, u32[]{:S(2)}, u32[]{:S(2)}) %collective-permute-start.37) | collective-permute-done | bytes 262176 | tf_op jit(solution)/shard_map/ppermute | solution.py:289
  311.5 29.2 %collective-permute-done.44.refs_22_ = bf16[64,16,128]{2,1,0:T(8,128)(2,1)S(1)} collective-permute-done((bf16[64,16,128]{2,1,0:T(8,128)(2,1)S(1)}, bf16[64,16,128]{2,1,0:T(8,128)(2,1)S(1)}, u32[]{:S(2)}, u32[]{:S(2)}) %collective-permute-start.44) | collective-permute-done | bytes 262176 | tf_op jit(solution)/shard_map/ppermute | solution.py:289
  344.8 7.2 collective-permute-done.45.refs_23_
  353.3 9.9 %collective-permute-done.46.refs_24_ = bf16[64,16,128]{2,1,0:T(8,128)(2,1)S(1)} collective-permute-done((bf16[64,16,128]{2,1,0:T(8,128)(2,1)S(1)}, bf16[64,16,128]{2,1,0:T(8,128)(2,1)S(1)}, u32[]{:S(2)}, u32[]{:S(2)}) %collective-permute-start.46) | collective-permute-done | bytes 262176 | tf_op jit(solution)/shard_map/ppermute | solution.py:289
  364.5 9.9 %collective-permute-done.47.refs_25_ = bf16[64,16,128]{2,1,0:T(8,128)(2,1)S(1)} collective-permute-done((bf16[64,16,128]{2,1,0:T(8,128)(2,1)S(1)}, bf16[64,16,128]{2,1,0:T(8,128)(2,1)S(1)}, u32[]{:S(2)}, u32[]{:S(2)}) %collective-permute-start.47) | collective-permute-done | bytes 262176 | tf_op jit(solution)/shard_map/ppermute | solution.py:289
  378.2 19.2 %collective-permute-start.33 = (bf16[64,16,128]{2,1,0:T(8,128)(2,1)S(1)}, bf16[64,16,128]{2,1,0:T(8,128)(2,1)S(1)}, u32[]{:S(2)}, u32[]{:S(2)}) collective-permute-start(bf16[64,16,128]{2,1,0:T(8,128)(2,1)S(1)} %get-tuple-element.174), channel_id=1, source_target_pairs={{0,1},{1,0},{2,3},{3,2},{4,5},{5,4},{6,7},{7,6},{8,9},{9,8},{10,11... | collective-permute-start | bytes 786440 | tf_op jit(solution)/shard_map/ppermute | solution.py:289
  405.4 20.1 %collective-permute-start.32 = (bf16[64,16,128]{2,1,0:T(8,128)(2,1)S(1)}, bf16[64,16,128]{2,1,0:T(8,128)(2,1)}, u32[]{:S(2)}, u32[]{:S(2)}) collective-permute-start(bf16[64,16,128]{2,1,0:T(8,128)(2,1)S(1)} %get-tuple-element.173), channel_id=1, source_target_pairs={{0,1},{1,0},{2,3},{3,2},{4,5},{5,4},{6,7},{7,6},{8,9},{9,8},{10,11... | collective-permute-start | bytes 786440 | tf_op jit(solution)/shard_map/ppermute | solution.py:289
  425.5 5.5 collective-permute-start.40
  436.6 10.9 %collective-permute-done.41.refs_19_ = bf16[64,16,128]{2,1,0:T(8,128)(2,1)S(1)} collective-permute-done((bf16[64,16,128]{2,1,0:T(8,128)(2,1)S(1)}, bf16[64,16,128]{2,1,0:T(8,128)(2,1)S(1)}, u32[]{:S(2)}, u32[]{:S(2)}) %collective-permute-start.41) | collective-permute-done | bytes 262176 | tf_op jit(solution)/shard_map/ppermute | solution.py:289
  447.5 11.3 %collective-permute-done.40.refs_18_ = bf16[64,16,128]{2,1,0:T(8,128)(2,1)} collective-permute-done((bf16[64,16,128]{2,1,0:T(8,128)(2,1)S(1)}, bf16[64,16,128]{2,1,0:T(8,128)(2,1)}, u32[]{:S(2)}, u32[]{:S(2)}) %collective-permute-start.40) | collective-permute-done | bytes 262176 | tf_op jit(solution)/shard_map/ppermute | solution.py:289
  458.9 14.7 %lines.1 = (bf16[64,16,128]{2,1,0:T(8,128)(2,1)S(1)}, bf16[64,16,128]{2,1,0:T(8,128)(2,1)S(1)}, bf16[64,16,128]{2,1,0:T(8,128)(2,1)S(1)}, bf16[64,16,128]{2,1,0:...) custom-call(s32[3]{0:T(128)S(1)} %pad_add_fusion.refs_0_, ...), custom_call_target="tpu_custom_call" | custom-call | flops 8589934592 | bytes 16777216 | tf_op jit(solution)/shard_map/lines/pallas_call | solution.py:216
  475.1 6.0 collective-permute-start.105
  485.1 7.6 collective-permute-done.105.refs_2_
  492.7 15.4 %collective-permute-done.106.refs_3_ = bf16[64,16,128]{2,1,0:T(8,128)(2,1)S(1)} collective-permute-done((bf16[64,16,128]{2,1,0:T(8,128)(2,1)S(1)}, bf16[64,16,128]{2,1,0:T(8,128)(2,1)S(1)}, u32[]{:S(2)}, u32[]{:S(2)}) %collective-permute-start.106) | collective-permute-done | bytes 262176 | tf_op jit(solution)/shard_map/ppermute | solution.py:289
  508.0 11.8 %collective-permute-start.92 = (bf16[64,16,128]{2,1,0:T(8,128)(2,1)S(1)}, bf16[64,16,128]{2,1,0:T(8,128)(2,1)S(1)}, u32[]{:S(2)}, u32[]{:S(2)}) collective-permute-start(bf16[64,16,128]{2,1,0:T(8,128)(2,1)S(1)} %get-tuple-element.239), channel_id=1, source_target_pairs={{0,2},{1,3},{2,0},{3,1},{4,6},{5,7},{6,4},{7,5},{8,10},{9,11},{10,... | collective-permute-start | bytes 786440 | tf_op jit(solution)/shard_map/ppermute | solution.py:289
  522.2 15.0 %collective-permute-start.84 = (bf16[64,16,128]{2,1,0:T(8,128)(2,1)S(1)}, bf16[64,16,128]{2,1,0:T(8,128)(2,1)S(1)}, u32[]{:S(2)}, u32[]{:S(2)}) collective-permute-start(bf16[64,16,128]{2,1,0:T(8,128)(2,1)S(1)} %get-tuple-element.230), channel_id=1, source_target_pairs={{0,1},{1,0},{2,3},{3,2},{4,5},{5,4},{6,7},{7,6},{8,9},{9,8},{10,11... | collective-permute-start | bytes 786440 | tf_op jit(solution)/shard_map/ppermute | solution.py:289
  543.3 15.4 %collective-permute-done.92.refs_3_ = bf16[64,16,128]{2,1,0:T(8,128)(2,1)S(1)} collective-permute-done((bf16[64,16,128]{2,1,0:T(8,128)(2,1)S(1)}, bf16[64,16,128]{2,1,0:T(8,128)(2,1)S(1)}, u32[]{:S(2)}, u32[]{:S(2)}) %collective-permute-start.92) | collective-permute-done | bytes 262176 | tf_op jit(solution)/shard_map/ppermute | solution.py:289
  558.6 6.1 collective-permute-start.78
  567.2 14.0 %collective-permute-done.85.refs_3_ = bf16[64,16,128]{2,1,0:T(8,128)(2,1)S(1)} collective-permute-done((bf16[64,16,128]{2,1,0:T(8,128)(2,1)S(1)}, bf16[64,16,128]{2,1,0:T(8,128)(2,1)S(1)}, u32[]{:S(2)}, u32[]{:S(2)}) %collective-permute-start.85) | collective-permute-done | bytes 262176 | tf_op jit(solution)/shard_map/ppermute | solution.py:289
  581.1 6.1 collective-permute-start.71
  589.7 14.0 %collective-permute-done.78.refs_3_ = bf16[64,16,128]{2,1,0:T(8,128)(2,1)S(1)} collective-permute-done((bf16[64,16,128]{2,1,0:T(8,128)(2,1)S(1)}, bf16[64,16,128]{2,1,0:T(8,128)(2,1)S(1)}, u32[]{:S(2)}, u32[]{:S(2)}) %collective-permute-start.78) | collective-permute-done | bytes 262176 | tf_op jit(solution)/shard_map/ppermute | solution.py:289
  603.7 6.1 collective-permute-start.64
  612.2 14.0 %collective-permute-done.71.refs_3_ = bf16[64,16,128]{2,1,0:T(8,128)(2,1)S(1)} collective-permute-done((bf16[64,16,128]{2,1,0:T(8,128)(2,1)S(1)}, bf16[64,16,128]{2,1,0:T(8,128)(2,1)S(1)}, u32[]{:S(2)}, u32[]{:S(2)}) %collective-permute-start.71) | collective-permute-done | bytes 262176 | tf_op jit(solution)/shard_map/ppermute | solution.py:289
  626.2 6.1 collective-permute-start.57
  637.1 11.6 %collective-permute-done.64.refs_3_ = bf16[64,16,128]{2,1,0:T(8,128)(2,1)S(1)} collective-permute-done((bf16[64,16,128]{2,1,0:T(8,128)(2,1)}, bf16[64,16,128]{2,1,0:T(8,128)(2,1)S(1)}, u32[]{:S(2)}, u32[]{:S(2)}) %collective-permute-start.64) | collective-permute-done | bytes 262176 | tf_op jit(solution)/shard_map/ppermute | solution.py:289
  653.0 7.0 collective-permute-done.57.refs_3_
  669.2 4.6 collective-permute-done.103.refs_4_
  680.4 4.7 collective-permute-done.96.refs_4_
  691.6 4.7 collective-permute-done.89.refs_4_
  727.9 4.8 collective-permute-done.68.refs_4_
  736.7 5.2 collective-permute-done.60.refs_3_
  757.2 16.6 %collective-permute-done.97.refs_6_ = bf16[16,256,128]{2,1,0:T(8,128)(2,1)S(1)} collective-permute-done((bf16[16,256,128]{2,1,0:T(8,128)(2,1)}, bf16[16,256,128]{2,1,0:T(8,128)(2,1)S(1)}, u32[]{:S(2)}, u32[]{:S(2)}) %collective-permute-start.97) | collective-permute-done | bytes 1048608 | tf_op jit(solution)/shard_map/ppermute | solution.py:289
  785.3 11.0 %collective-permute-done.90.refs_6_ = bf16[16,256,128]{2,1,0:T(8,128)(2,1)} collective-permute-done((bf16[16,256,128]{2,1,0:T(8,128)(2,1)}, bf16[16,256,128]{2,1,0:T(8,128)(2,1)}, u32[]{:S(2)}, u32[]{:S(2)}) %collective-permute-start.90) | collective-permute-done | bytes 1048608 | tf_op jit(solution)/shard_map/ppermute | solution.py:289
  799.5 19.3 %collective-permute-done.83.refs_6_ = bf16[16,256,128]{2,1,0:T(8,128)(2,1)S(1)} collective-permute-done((bf16[16,256,128]{2,1,0:T(8,128)(2,1)}, bf16[16,256,128]{2,1,0:T(8,128)(2,1)S(1)}, u32[]{:S(2)}, u32[]{:S(2)}) %collective-permute-start.83) | collective-permute-done | bytes 1048608 | tf_op jit(solution)/shard_map/ppermute | solution.py:289
  820.8 20.4 %collective-permute-done.76.refs_6_ = bf16[16,256,128]{2,1,0:T(8,128)(2,1)S(1)} collective-permute-done((bf16[16,256,128]{2,1,0:T(8,128)(2,1)}, bf16[16,256,128]{2,1,0:T(8,128)(2,1)S(1)}, u32[]{:S(2)}, u32[]{:S(2)}) %collective-permute-start.76) | collective-permute-done | bytes 1048608 | tf_op jit(solution)/shard_map/ppermute | solution.py:289
  843.3 20.4 %collective-permute-done.69.refs_6_ = bf16[16,256,128]{2,1,0:T(8,128)(2,1)S(1)} collective-permute-done((bf16[16,256,128]{2,1,0:T(8,128)(2,1)}, bf16[16,256,128]{2,1,0:T(8,128)(2,1)S(1)}, u32[]{:S(2)}, u32[]{:S(2)}) %collective-permute-start.69) | collective-permute-done | bytes 1048608 | tf_op jit(solution)/shard_map/ppermute | solution.py:289
  865.7 18.6 %collective-permute-done.62.refs_6_ = bf16[16,256,128]{2,1,0:T(8,128)(2,1)S(1)} collective-permute-done((bf16[16,256,128]{2,1,0:T(8,128)(2,1)}, bf16[16,256,128]{2,1,0:T(8,128)(2,1)S(1)}, u32[]{:S(2)}, u32[]{:S(2)}) %collective-permute-start.62) | collective-permute-done | bytes 1048608 | tf_op jit(solution)/shard_map/ppermute | solution.py:289
  (333 shorter events, 288.4 us)
Async XLA Ops:
  5.6 45.2 %collective-permute-start.12 = (bf16[16,256,128]{2,1,0:T(8,128)(2,1)S(1)}, bf16[16,256,128]{2,1,0:T(8,128)(2,1)S(1)}, u32[]{:S(2)}, u32[]{:S(2)}) collective-permute-start(bf16[16,256,128]{2,1,0:T(8,128)(2,1)S(1)} %copy_rows.11), channel_id=1, source_target_pairs={{0,16},{16,0},{1,17},{17,1},{2,18},{18,2},{3,19},{19,3},{4,20},{20... | collective-permute-start | bytes 3145736 | tf_op jit(solution)/shard_map/ppermute | solution.py:289
  6.9 66.3 %collective-permute-start.16 = (bf16[16,256,128]{2,1,0:T(8,128)(2,1)S(1)}, bf16[16,256,128]{2,1,0:T(8,128)(2,1)S(1)}, u32[]{:S(2)}, u32[]{:S(2)}) collective-permute-start(bf16[16,256,128]{2,1,0:T(8,128)(2,1)S(1)} %copy_rows.12), channel_id=1, source_target_pairs={{0,16},{16,0},{1,17},{17,1},{2,18},{18,2},{3,19},{19,3},{4,20},{20... | collective-permute-start | bytes 3145736 | tf_op jit(solution)/shard_map/ppermute | solution.py:289
  11.1 84.8 %collective-permute-start.20 = (bf16[16,256,128]{2,1,0:T(8,128)(2,1)}, bf16[16,256,128]{2,1,0:T(8,128)(2,1)}, u32[]{:S(2)}, u32[]{:S(2)}) collective-permute-start(bf16[16,256,128]{2,1,0:T(8,128)(2,1)} %copy_rows.13), channel_id=1, source_target_pairs={{0,16},{16,0},{1,17},{17,1},{2,18},{18,2},{3,19},{19,3},{4,20},{20... | collective-permute-start | bytes 3145736 | tf_op jit(solution)/shard_map/ppermute | solution.py:289
  13.2 105.1 %collective-permute-start.24 = (bf16[16,256,128]{2,1,0:T(8,128)(2,1)}, bf16[16,256,128]{2,1,0:T(8,128)(2,1)}, u32[]{:S(2)}, u32[]{:S(2)}) collective-permute-start(bf16[16,256,128]{2,1,0:T(8,128)(2,1)} %copy_rows.14), channel_id=1, source_target_pairs={{0,16},{16,0},{1,17},{17,1},{2,18},{18,2},{3,19},{19,3},{4,20},{20... | collective-permute-start | bytes 3145736 | tf_op jit(solution)/shard_map/ppermute | solution.py:289
  28.3 112.5 %collective-permute-start.28 = (bf16[16,256,128]{2,1,0:T(8,128)(2,1)}, bf16[16,256,128]{2,1,0:T(8,128)(2,1)}, u32[]{:S(2)}, u32[]{:S(2)}) collective-permute-start(bf16[16,256,128]{2,1,0:T(8,128)(2,1)} %copy_rows.15), channel_id=1, source_target_pairs={{0,16},{16,0},{1,17},{17,1},{2,18},{18,2},{3,19},{19,3},{4,20},{20... | collective-permute-start | bytes 3145736 | tf_op jit(solution)/shard_map/ppermute | solution.py:289
  50.8 112.4 %collective-permute-start.4 = (bf16[16,256,128]{2,1,0:T(8,128)(2,1)}, bf16[16,256,128]{2,1,0:T(8,128)(2,1)S(1)}, u32[]{:S(2)}, u32[]{:S(2)}) collective-permute-start(bf16[16,256,128]{2,1,0:T(8,128)(2,1)} %copy_rows.9), channel_id=1, source_target_pairs={{0,16},{16,0},{1,17},{17,1},{2,18},{18,2},{3,19},{19,3},{4,20},{20... | collective-permute-start | bytes 3145736 | tf_op jit(solution)/shard_map/ppermute | solution.py:289
  74.2 110.5 %collective-permute-start = (bf16[16,256,128]{2,1,0:T(8,128)(2,1)}, bf16[16,256,128]{2,1,0:T(8,128)(2,1)S(1)}, u32[]{:S(2)}, u32[]{:S(2)}) collective-permute-start(bf16[16,256,128]{2,1,0:T(8,128)(2,1)} %copy_rows.8), channel_id=1, source_target_pairs={{0,16},{16,0},{1,17},{17,1},{2,18},{18,2},{3,19},{19,3},{4,20},{20... | collective-permute-start | bytes 3145736 | tf_op jit(solution)/shard_map/ppermute | solution.py:289
  95.9 90.6 %collective-permute-start.10 = (bf16[16,64,128]{2,1,0:T(8,128)(2,1)S(1)}, bf16[16,64,128]{2,1,0:T(8,128)(2,1)S(1)}, u32[]{:S(2)}, u32[]{:S(2)}) collective-permute-start(bf16[16,64,128]{2,1,0:T(8,128)(2,1)S(1)} %get-tuple-element.145), channel_id=1, source_target_pairs={{0,8},{4,12},{8,0},{12,4},{1,9},{5,13},{9,1},{13,5},{2,10},{6,14},... | collective-permute-start | bytes 786440 | tf_op jit(solution)/shard_map/ppermute | solution.py:289
  118.3 68.2 %collective-permute-start.11 = (bf16[16,64,128]{2,1,0:T(8,128)(2,1)S(1)}, bf16[16,64,128]{2,1,0:T(8,128)(2,1)S(1)}, u32[]{:S(2)}, u32[]{:S(2)}) collective-permute-start(bf16[16,64,128]{2,1,0:T(8,128)(2,1)S(1)} %get-tuple-element.146), channel_id=1, source_target_pairs={{0,12},{4,8},{8,4},{12,0},{1,13},{5,9},{9,5},{13,1},{2,14},{6,10},... | collective-permute-start | bytes 786440 | tf_op jit(solution)/shard_map/ppermute | solution.py:289
  140.8 46.1 %collective-permute-start.9 = (bf16[16,64,128]{2,1,0:T(8,128)(2,1)S(1)}, bf16[16,64,128]{2,1,0:T(8,128)(2,1)S(1)}, u32[]{:S(2)}, u32[]{:S(2)}) collective-permute-start(bf16[16,64,128]{2,1,0:T(8,128)(2,1)S(1)} %get-tuple-element.144), channel_id=1, source_target_pairs={{0,4},{4,0},{8,12},{12,8},{1,5},{5,1},{9,13},{13,9},{2,6},{6,2},{1... | collective-permute-start | bytes 786440 | tf_op jit(solution)/shard_map/ppermute | solution.py:289
  268.1 37.0 %collective-permute-start.39 = (bf16[64,16,128]{2,1,0:T(8,128)(2,1)S(1)}, bf16[64,16,128]{2,1,0:T(8,128)(2,1)S(1)}, u32[]{:S(2)}, u32[]{:S(2)}) collective-permute-start(bf16[64,16,128]{2,1,0:T(8,128)(2,1)S(1)} %get-tuple-element.180), channel_id=1, source_target_pairs={{0,1},{1,0},{2,3},{3,2},{4,5},{5,4},{6,7},{7,6},{8,9},{9,8},{10,11... | collective-permute-start | bytes 786440 | tf_op jit(solution)/shard_map/ppermute | solution.py:289
  271.9 34.7 %collective-permute-start.42 = (bf16[64,16,128]{2,1,0:T(8,128)(2,1)S(1)}, bf16[64,16,128]{2,1,0:T(8,128)(2,1)S(1)}, u32[]{:S(2)}, u32[]{:S(2)}) collective-permute-start(bf16[64,16,128]{2,1,0:T(8,128)(2,1)S(1)} %get-tuple-element.183), channel_id=1, source_target_pairs={{0,2},{1,3},{2,0},{3,1},{4,6},{5,7},{6,4},{7,5},{8,10},{9,11},{10,... | collective-permute-start | bytes 786440 | tf_op jit(solution)/shard_map/ppermute | solution.py:289
  294.4 46.3 %collective-permute-start.44 = (bf16[64,16,128]{2,1,0:T(8,128)(2,1)S(1)}, bf16[64,16,128]{2,1,0:T(8,128)(2,1)S(1)}, u32[]{:S(2)}, u32[]{:S(2)}) collective-permute-start(bf16[64,16,128]{2,1,0:T(8,128)(2,1)S(1)} %get-tuple-element.185), channel_id=1, source_target_pairs={{0,2},{1,3},{2,0},{3,1},{4,6},{5,7},{6,4},{7,5},{8,10},{9,11},{10,... | collective-permute-start | bytes 786440 | tf_op jit(solution)/shard_map/ppermute | solution.py:289
  300.2 51.7 %collective-permute-start.45 = (bf16[64,16,128]{2,1,0:T(8,128)(2,1)S(1)}, bf16[64,16,128]{2,1,0:T(8,128)(2,1)S(1)}, u32[]{:S(2)}, u32[]{:S(2)}) collective-permute-start(bf16[64,16,128]{2,1,0:T(8,128)(2,1)S(1)} %get-tuple-element.186), channel_id=1, source_target_pairs={{0,2},{1,3},{2,0},{3,1},{4,6},{5,7},{6,4},{7,5},{8,10},{9,11},{10,... | collective-permute-start | bytes 786440 | tf_op jit(solution)/shard_map/ppermute | solution.py:289
  305.1 58.1 %collective-permute-start.46 = (bf16[64,16,128]{2,1,0:T(8,128)(2,1)S(1)}, bf16[64,16,128]{2,1,0:T(8,128)(2,1)S(1)}, u32[]{:S(2)}, u32[]{:S(2)}) collective-permute-start(bf16[64,16,128]{2,1,0:T(8,128)(2,1)S(1)} %get-tuple-element.187), channel_id=1, source_target_pairs={{0,2},{1,3},{2,0},{3,1},{4,6},{5,7},{6,4},{7,5},{8,10},{9,11},{10,... | collective-permute-start | bytes 786440 | tf_op jit(solution)/shard_map/ppermute | solution.py:289
  306.7 67.7 %collective-permute-start.47 = (bf16[64,16,128]{2,1,0:T(8,128)(2,1)S(1)}, bf16[64,16,128]{2,1,0:T(8,128)(2,1)S(1)}, u32[]{:S(2)}, u32[]{:S(2)}) collective-permute-start(bf16[64,16,128]{2,1,0:T(8,128)(2,1)S(1)} %get-tuple-element.188), channel_id=1, source_target_pairs={{0,2},{1,3},{2,0},{3,1},{4,6},{5,7},{6,4},{7,5},{8,10},{9,11},{10,... | collective-permute-start | bytes 786440 | tf_op jit(solution)/shard_map/ppermute | solution.py:289
  308.0 67.8 %collective-permute-start.50 = (bf16[64,16,128]{2,1,0:T(8,128)(2,1)S(1)}, bf16[64,16,128]{2,1,0:T(8,128)(2,1)S(1)}, u32[]{:S(2)}, u32[]{:S(2)}) collective-permute-start(bf16[64,16,128]{2,1,0:T(8,128)(2,1)S(1)} %get-tuple-element.191), channel_id=1, source_target_pairs={{0,3},{1,2},{2,1},{3,0},{4,7},{5,6},{6,5},{7,4},{8,11},{9,10},{10,... | collective-permute-start | bytes 786440 | tf_op jit(solution)/shard_map/ppermute | solution.py:289
  340.7 37.5 %collective-permute-start.51 = (bf16[64,16,128]{2,1,0:T(8,128)(2,1)S(1)}, bf16[64,16,128]{2,1,0:T(8,128)(2,1)S(1)}, u32[]{:S(2)}, u32[]{:S(2)}) collective-permute-start(bf16[64,16,128]{2,1,0:T(8,128)(2,1)S(1)} %get-tuple-element.192), channel_id=1, source_target_pairs={{0,3},{1,2},{2,1},{3,0},{4,7},{5,6},{6,5},{7,4},{8,11},{9,10},{10,... | collective-permute-start | bytes 786440 | tf_op jit(solution)/shard_map/ppermute | solution.py:289
  351.9 48.7 %collective-permute-start.52 = (bf16[64,16,128]{2,1,0:T(8,128)(2,1)S(1)}, bf16[64,16,128]{2,1,0:T(8,128)(2,1)S(1)}, u32[]{:S(2)}, u32[]{:S(2)}) collective-permute-start(bf16[64,16,128]{2,1,0:T(8,128)(2,1)S(1)} %get-tuple-element.193), channel_id=1, source_target_pairs={{0,3},{1,2},{2,1},{3,0},{4,7},{5,6},{6,5},{7,4},{8,11},{9,10},{10,... | collective-permute-start | bytes 786440 | tf_op jit(solution)/shard_map/ppermute | solution.py:289
  363.2 39.8 %collective-permute-start.53 = (bf16[64,16,128]{2,1,0:T(8,128)(2,1)S(1)}, bf16[64,16,128]{2,1,0:T(8,128)(2,1)S(1)}, u32[]{:S(2)}, u32[]{:S(2)}) collective-permute-start(bf16[64,16,128]{2,1,0:T(8,128)(2,1)S(1)} %get-tuple-element.194), channel_id=1, source_target_pairs={{0,3},{1,2},{2,1},{3,0},{4,7},{5,6},{6,5},{7,4},{8,11},{9,10},{10,... | collective-permute-start | bytes 786440 | tf_op jit(solution)/shard_map/ppermute | solution.py:289
  375.8 49.8 %collective-permute-start.55 = (bf16[64,16,128]{2,1,0:T(8,128)(2,1)S(1)}, bf16[64,16,128]{2,1,0:T(8,128)(2,1)S(1)}, u32[]{:S(2)}, u32[]{:S(2)}) collective-permute-start(bf16[64,16,128]{2,1,0:T(8,128)(2,1)S(1)} %get-tuple-element.196), channel_id=1, source_target_pairs={{0,3},{1,2},{2,1},{3,0},{4,7},{5,6},{6,5},{7,4},{8,11},{9,10},{10,... | collective-permute-start | bytes 786440 | tf_op jit(solution)/shard_map/ppermute | solution.py:289
  378.2 52.8 %collective-permute-start.33 = (bf16[64,16,128]{2,1,0:T(8,128)(2,1)S(1)}, bf16[64,16,128]{2,1,0:T(8,128)(2,1)S(1)}, u32[]{:S(2)}, u32[]{:S(2)}) collective-permute-start(bf16[64,16,128]{2,1,0:T(8,128)(2,1)S(1)} %get-tuple-element.174), channel_id=1, source_target_pairs={{0,1},{1,0},{2,3},{3,2},{4,5},{5,4},{6,7},{7,6},{8,9},{9,8},{10,11... | collective-permute-start | bytes 786440 | tf_op jit(solution)/shard_map/ppermute | solution.py:289
  400.7 46.8 %collective-permute-start.41 = (bf16[64,16,128]{2,1,0:T(8,128)(2,1)S(1)}, bf16[64,16,128]{2,1,0:T(8,128)(2,1)S(1)}, u32[]{:S(2)}, u32[]{:S(2)}) collective-permute-start(bf16[64,16,128]{2,1,0:T(8,128)(2,1)S(1)} %get-tuple-element.182), channel_id=1, source_target_pairs={{0,2},{1,3},{2,0},{3,1},{4,6},{5,7},{6,4},{7,5},{8,10},{9,11},{10,... | collective-permute-start | bytes 786440 | tf_op jit(solution)/shard_map/ppermute | solution.py:289
  403.0 44.5 %collective-permute-start.49 = (bf16[64,16,128]{2,1,0:T(8,128)(2,1)S(1)}, bf16[64,16,128]{2,1,0:T(8,128)(2,1)S(1)}, u32[]{:S(2)}, u32[]{:S(2)}) collective-permute-start(bf16[64,16,128]{2,1,0:T(8,128)(2,1)S(1)} %get-tuple-element.190), channel_id=1, source_target_pairs={{0,3},{1,2},{2,1},{3,0},{4,7},{5,6},{6,5},{7,4},{8,11},{9,10},{10,... | collective-permute-start | bytes 786440 | tf_op jit(solution)/shard_map/ppermute | solution.py:289
  405.4 42.1 %collective-permute-start.32 = (bf16[64,16,128]{2,1,0:T(8,128)(2,1)S(1)}, bf16[64,16,128]{2,1,0:T(8,128)(2,1)}, u32[]{:S(2)}, u32[]{:S(2)}) collective-permute-start(bf16[64,16,128]{2,1,0:T(8,128)(2,1)S(1)} %get-tuple-element.173), channel_id=1, source_target_pairs={{0,1},{1,0},{2,3},{3,2},{4,5},{5,4},{6,7},{7,6},{8,9},{9,8},{10,11... | collective-permute-start | bytes 786440 | tf_op jit(solution)/shard_map/ppermute | solution.py:289
  483.4 36.4 %collective-permute-start.100 = (bf16[64,16,128]{2,1,0:T(8,128)(2,1)}, bf16[64,16,128]{2,1,0:T(8,128)(2,1)S(1)}, u32[]{:S(2)}, u32[]{:S(2)}) collective-permute-start(bf16[64,16,128]{2,1,0:T(8,128)(2,1)} %get-tuple-element.248), channel_id=1, source_target_pairs={{0,3},{1,2},{2,1},{3,0},{4,7},{5,6},{6,5},{7,4},{8,11},{9,10},{10,... | collective-permute-start | bytes 786440 | tf_op jit(solution)/shard_map/ppermute | solution.py:289
  484.9 37.3 %collective-permute-start.98 = (bf16[64,16,128]{2,1,0:T(8,128)(2,1)S(1)}, bf16[64,16,128]{2,1,0:T(8,128)(2,1)S(1)}, u32[]{:S(2)}, u32[]{:S(2)}) collective-permute-start(bf16[64,16,128]{2,1,0:T(8,128)(2,1)S(1)} %get-tuple-element.246), channel_id=1, source_target_pairs={{0,1},{1,0},{2,3},{3,2},{4,5},{5,4},{6,7},{7,6},{8,9},{9,8},{10,11... | collective-permute-start | bytes 786440 | tf_op jit(solution)/shard_map/ppermute | solution.py:289
  492.6 49.2 %collective-permute-start.99 = (bf16[64,16,128]{2,1,0:T(8,128)(2,1)S(1)}, bf16[64,16,128]{2,1,0:T(8,128)(2,1)S(1)}, u32[]{:S(2)}, u32[]{:S(2)}) collective-permute-start(bf16[64,16,128]{2,1,0:T(8,128)(2,1)S(1)} %get-tuple-element.247), channel_id=1, source_target_pairs={{0,2},{1,3},{2,0},{3,1},{4,6},{5,7},{6,4},{7,5},{8,10},{9,11},{10,... | collective-permute-start | bytes 786440 | tf_op jit(solution)/shard_map/ppermute | solution.py:289
  508.0 33.8 %collective-permute-start.91 = (bf16[64,16,128]{2,1,0:T(8,128)(2,1)S(1)}, bf16[64,16,128]{2,1,0:T(8,128)(2,1)S(1)}, u32[]{:S(2)}, u32[]{:S(2)}) collective-permute-start(bf16[64,16,128]{2,1,0:T(8,128)(2,1)S(1)} %get-tuple-element.238), channel_id=1, source_target_pairs={{0,1},{1,0},{2,3},{3,2},{4,5},{5,4},{6,7},{7,6},{8,9},{9,8},{10,11... | collective-permute-start | bytes 786440 | tf_op jit(solution)/shard_map/ppermute | solution.py:289
  508.0 50.6 %collective-permute-start.92 = (bf16[64,16,128]{2,1,0:T(8,128)(2,1)S(1)}, bf16[64,16,128]{2,1,0:T(8,128)(2,1)S(1)}, u32[]{:S(2)}, u32[]{:S(2)}) collective-permute-start(bf16[64,16,128]{2,1,0:T(8,128)(2,1)S(1)} %get-tuple-element.239), channel_id=1, source_target_pairs={{0,2},{1,3},{2,0},{3,1},{4,6},{5,7},{6,4},{7,5},{8,10},{9,11},{10,... | collective-permute-start | bytes 786440 | tf_op jit(solution)/shard_map/ppermute | solution.py:289
  519.8 38.8 %collective-permute-start.93 = (bf16[64,16,128]{2,1,0:T(8,128)(2,1)}, bf16[64,16,128]{2,1,0:T(8,128)(2,1)S(1)}, u32[]{:S(2)}, u32[]{:S(2)}) collective-permute-start(bf16[64,16,128]{2,1,0:T(8,128)(2,1)} %get-tuple-element.240), channel_id=1, source_target_pairs={{0,3},{1,2},{2,1},{3,0},{4,7},{5,6},{6,5},{7,4},{8,11},{9,10},{10,... | collective-permute-start | bytes 786440 | tf_op jit(solution)/shard_map/ppermute | solution.py:289
  522.2 42.6 %collective-permute-start.84 = (bf16[64,16,128]{2,1,0:T(8,128)(2,1)S(1)}, bf16[64,16,128]{2,1,0:T(8,128)(2,1)S(1)}, u32[]{:S(2)}, u32[]{:S(2)}) collective-permute-start(bf16[64,16,128]{2,1,0:T(8,128)(2,1)S(1)} %get-tuple-element.230), channel_id=1, source_target_pairs={{0,1},{1,0},{2,3},{3,2},{4,5},{5,4},{6,7},{7,6},{8,9},{9,8},{10,11... | collective-permute-start | bytes 786440 | tf_op jit(solution)/shard_map/ppermute | solution.py:289
  541.8 39.3 %collective-permute-start.85 = (bf16[64,16,128]{2,1,0:T(8,128)(2,1)S(1)}, bf16[64,16,128]{2,1,0:T(8,128)(2,1)S(1)}, u32[]{:S(2)}, u32[]{:S(2)}) collective-permute-start(bf16[64,16,128]{2,1,0:T(8,128)(2,1)S(1)} %get-tuple-element.231), channel_id=1, source_target_pairs={{0,2},{1,3},{2,0},{3,1},{4,6},{5,7},{6,4},{7,5},{8,10},{9,11},{10,... | collective-permute-start | bytes 786440 | tf_op jit(solution)/shard_map/ppermute | solution.py:289
  541.8 39.3 %collective-permute-start.86 = (bf16[64,16,128]{2,1,0:T(8,128)(2,1)}, bf16[64,16,128]{2,1,0:T(8,128)(2,1)S(1)}, u32[]{:S(2)}, u32[]{:S(2)}) collective-permute-start(bf16[64,16,128]{2,1,0:T(8,128)(2,1)} %get-tuple-element.232), channel_id=1, source_target_pairs={{0,3},{1,2},{2,1},{3,0},{4,7},{5,6},{6,5},{7,4},{8,11},{9,10},{10,... | collective-permute-start | bytes 786440 | tf_op jit(solution)/shard_map/ppermute | solution.py:289
  558.6 45.0 %collective-permute-start.78 = (bf16[64,16,128]{2,1,0:T(8,128)(2,1)S(1)}, bf16[64,16,128]{2,1,0:T(8,128)(2,1)S(1)}, u32[]{:S(2)}, u32[]{:S(2)}) collective-permute-start(bf16[64,16,128]{2,1,0:T(8,128)(2,1)S(1)} %get-tuple-element.223), channel_id=1, source_target_pairs={{0,2},{1,3},{2,0},{3,1},{4,6},{5,7},{6,4},{7,5},{8,10},{9,11},{10,... | collective-permute-start | bytes 786440 | tf_op jit(solution)/shard_map/ppermute | solution.py:289
  564.8 38.9 %collective-permute-start.79 = (bf16[64,16,128]{2,1,0:T(8,128)(2,1)}, bf16[64,16,128]{2,1,0:T(8,128)(2,1)S(1)}, u32[]{:S(2)}, u32[]{:S(2)}) collective-permute-start(bf16[64,16,128]{2,1,0:T(8,128)(2,1)} %get-tuple-element.224), channel_id=1, source_target_pairs={{0,3},{1,2},{2,1},{3,0},{4,7},{5,6},{6,5},{7,4},{8,11},{9,10},{10,... | collective-permute-start | bytes 786440 | tf_op jit(solution)/shard_map/ppermute | solution.py:289
  581.1 45.0 %collective-permute-start.71 = (bf16[64,16,128]{2,1,0:T(8,128)(2,1)S(1)}, bf16[64,16,128]{2,1,0:T(8,128)(2,1)S(1)}, u32[]{:S(2)}, u32[]{:S(2)}) collective-permute-start(bf16[64,16,128]{2,1,0:T(8,128)(2,1)S(1)} %get-tuple-element.215), channel_id=1, source_target_pairs={{0,2},{1,3},{2,0},{3,1},{4,6},{5,7},{6,4},{7,5},{8,10},{9,11},{10,... | collective-permute-start | bytes 786440 | tf_op jit(solution)/shard_map/ppermute | solution.py:289
  587.3 38.9 %collective-permute-start.72 = (bf16[64,16,128]{2,1,0:T(8,128)(2,1)}, bf16[64,16,128]{2,1,0:T(8,128)(2,1)S(1)}, u32[]{:S(2)}, u32[]{:S(2)}) collective-permute-start(bf16[64,16,128]{2,1,0:T(8,128)(2,1)} %get-tuple-element.216), channel_id=1, source_target_pairs={{0,3},{1,2},{2,1},{3,0},{4,7},{5,6},{6,5},{7,4},{8,11},{9,10},{10,... | collective-permute-start | bytes 786440 | tf_op jit(solution)/shard_map/ppermute | solution.py:289
  603.7 45.0 %collective-permute-start.64 = (bf16[64,16,128]{2,1,0:T(8,128)(2,1)}, bf16[64,16,128]{2,1,0:T(8,128)(2,1)S(1)}, u32[]{:S(2)}, u32[]{:S(2)}) collective-permute-start(bf16[64,16,128]{2,1,0:T(8,128)(2,1)} %get-tuple-element.207), channel_id=1, source_target_pairs={{0,2},{1,3},{2,0},{3,1},{4,6},{5,7},{6,4},{7,5},{8,10},{9,11},{10,... | collective-permute-start | bytes 786440 | tf_op jit(solution)/shard_map/ppermute | solution.py:289
  609.8 38.9 %collective-permute-start.65 = (bf16[64,16,128]{2,1,0:T(8,128)(2,1)}, bf16[64,16,128]{2,1,0:T(8,128)(2,1)S(1)}, u32[]{:S(2)}, u32[]{:S(2)}) collective-permute-start(bf16[64,16,128]{2,1,0:T(8,128)(2,1)} %get-tuple-element.208), channel_id=1, source_target_pairs={{0,3},{1,2},{2,1},{3,0},{4,7},{5,6},{6,5},{7,4},{8,11},{9,10},{10,... | collective-permute-start | bytes 786440 | tf_op jit(solution)/shard_map/ppermute | solution.py:289
  702.8 47.2 %collective-permute-start.111 = (bf16[16,256,128]{2,1,0:T(8,128)(2,1)S(1)}, bf16[16,256,128]{2,1,0:T(8,128)(2,1)S(1)}, u32[]{:S(2)}, u32[]{:S(2)}) collective-permute-start(bf16[16,256,128]{2,1,0:T(8,128)(2,1)S(1)} %inverse_y.23), channel_id=1, source_target_pairs={{0,16},{16,0},{1,17},{17,1},{2,18},{18,2},{3,19},{19,3},{4,20},{20... | collective-permute-start | bytes 3145736 | tf_op jit(solution)/shard_map/ppermute | solution.py:289
  707.5 46.3 %collective-permute-start.104 = (bf16[16,256,128]{2,1,0:T(8,128)(2,1)S(1)}, bf16[16,256,128]{2,1,0:T(8,128)(2,1)S(1)}, u32[]{:S(2)}, u32[]{:S(2)}) collective-permute-start(bf16[16,256,128]{2,1,0:T(8,128)(2,1)S(1)} %inverse_y.22), channel_id=1, source_target_pairs={{0,16},{16,0},{1,17},{17,1},{2,18},{18,2},{3,19},{19,3},{4,20},{20... | collective-permute-start | bytes 3145736 | tf_op jit(solution)/shard_map/ppermute | solution.py:289
  710.9 62.9 %collective-permute-start.97 = (bf16[16,256,128]{2,1,0:T(8,128)(2,1)}, bf16[16,256,128]{2,1,0:T(8,128)(2,1)S(1)}, u32[]{:S(2)}, u32[]{:S(2)}) collective-permute-start(bf16[16,256,128]{2,1,0:T(8,128)(2,1)} %inverse_y.21), channel_id=1, source_target_pairs={{0,16},{16,0},{1,17},{17,1},{2,18},{18,2},{3,19},{19,3},{4,20},{20... | collective-permute-start | bytes 3145736 | tf_op jit(solution)/shard_map/ppermute | solution.py:289
  741.9 54.4 %collective-permute-start.90 = (bf16[16,256,128]{2,1,0:T(8,128)(2,1)}, bf16[16,256,128]{2,1,0:T(8,128)(2,1)}, u32[]{:S(2)}, u32[]{:S(2)}) collective-permute-start(bf16[16,256,128]{2,1,0:T(8,128)(2,1)} %inverse_y.20), channel_id=1, source_target_pairs={{0,16},{16,0},{1,17},{17,1},{2,18},{18,2},{3,19},{19,3},{4,20},{20... | collective-permute-start | bytes 3145736 | tf_op jit(solution)/shard_map/ppermute | solution.py:289
  746.6 72.1 %collective-permute-start.83 = (bf16[16,256,128]{2,1,0:T(8,128)(2,1)}, bf16[16,256,128]{2,1,0:T(8,128)(2,1)S(1)}, u32[]{:S(2)}, u32[]{:S(2)}) collective-permute-start(bf16[16,256,128]{2,1,0:T(8,128)(2,1)} %inverse_y.19), channel_id=1, source_target_pairs={{0,16},{16,0},{1,17},{17,1},{2,18},{18,2},{3,19},{19,3},{4,20},{20... | collective-permute-start | bytes 3145736 | tf_op jit(solution)/shard_map/ppermute | solution.py:289
  751.0 90.3 %collective-permute-start.76 = (bf16[16,256,128]{2,1,0:T(8,128)(2,1)}, bf16[16,256,128]{2,1,0:T(8,128)(2,1)S(1)}, u32[]{:S(2)}, u32[]{:S(2)}) collective-permute-start(bf16[16,256,128]{2,1,0:T(8,128)(2,1)} %inverse_y.18), channel_id=1, source_target_pairs={{0,16},{16,0},{1,17},{17,1},{2,18},{18,2},{3,19},{19,3},{4,20},{20... | collective-permute-start | bytes 3145736 | tf_op jit(solution)/shard_map/ppermute | solution.py:289
  753.8 109.8 %collective-permute-start.69 = (bf16[16,256,128]{2,1,0:T(8,128)(2,1)}, bf16[16,256,128]{2,1,0:T(8,128)(2,1)S(1)}, u32[]{:S(2)}, u32[]{:S(2)}) collective-permute-start(bf16[16,256,128]{2,1,0:T(8,128)(2,1)} %inverse_y.17), channel_id=1, source_target_pairs={{0,16},{16,0},{1,17},{17,1},{2,18},{18,2},{3,19},{19,3},{4,20},{20... | collective-permute-start | bytes 3145736 | tf_op jit(solution)/shard_map/ppermute | solution.py:289
  773.8 110.6 %collective-permute-start.62 = (bf16[16,256,128]{2,1,0:T(8,128)(2,1)}, bf16[16,256,128]{2,1,0:T(8,128)(2,1)S(1)}, u32[]{:S(2)}, u32[]{:S(2)}) collective-permute-start(bf16[16,256,128]{2,1,0:T(8,128)(2,1)} %inverse_y.16), channel_id=1, source_target_pairs={{0,16},{16,0},{1,17},{17,1},{2,18},{18,2},{3,19},{19,3},{4,20},{20... | collective-permute-start | bytes 3145736 | tf_op jit(solution)/shard_map/ppermute | solution.py:289
  (116 other events, 4349.9 us)
